TPU v7x, 128 devices: a whole 4x4x4 slice. The times are simulated.
128 devices in a mesh: emb: 4 (over z), col: 4 (over y), row: 8 (over x, core).
Axes of the slice: x: 4, y: 4, z: 4, core: 2. Of those that a mesh axis runs over, the one named last changes fastest.
Arguments:
- inter_mask: int32 [2048, 65536], P('row', 'col')
- emb_user: bfloat16 [2048, 64], P(('row', 'col'), 'emb')
- emb_item: bfloat16 [65536, 64], P(('col', 'row'), 'emb')
- triples: int32 [4096, 3], replicated
Outputs:
- output 1: bfloat16 [2048, 64], P(('row', 'col'), 'emb')
- output 2: bfloat16 [65536, 64], P(('col', 'row'), 'emb')
- output 3: float32 [4096], replicated
All inputs are finite; a program needn't handle non-finite values.
Results may differ from a plain program's by a relative error of at most 0.0107327.
Values are sent between devices in bfloat16 or wider.
A program may use at most 1 GiB of HBM per device.

v0:
```python
import jax
import jax.numpy as jnp
from jax import lax
from jax.sharding import PartitionSpec as P

NUM_LAYERS = 3


def lookup_rows(table, ids, offset):
    own_rows = table.shape[0]
    local_ids = ids - offset
    owned = (local_ids >= 0) & (local_ids < own_rows)
    picked = jnp.take(table, jnp.clip(local_ids, 0, own_rows - 1), axis=0)
    return jnp.where(owned[:, None], picked.astype(jnp.float32), 0.0)


def bpr_terms(final_user, final_item, triples, user_off, item_off):
    num_trip = triples.shape[0]
    fetched = jnp.concatenate([
        lookup_rows(final_user, triples[:, 0], user_off),
        lookup_rows(final_item, triples[:, 1], item_off),
        lookup_rows(final_item, triples[:, 2], item_off)], axis=0)
    fetched = lax.psum(fetched, ("row", "col"))
    e_user = fetched[:num_trip]
    e_pos = fetched[num_trip:2 * num_trip]
    e_neg = fetched[2 * num_trip:]
    score = lax.psum(jnp.sum(e_user * (e_pos - e_neg), axis=1), "emb")
    return jax.nn.softplus(-score)


def norm_adjacency(mask_blk):
    deg_user = lax.psum(jnp.sum(mask_blk, axis=1), "col")
    deg_item = lax.psum(jnp.sum(mask_blk, axis=0), "row")
    inv_user = lax.rsqrt(jnp.maximum(deg_user, 1).astype(jnp.float32))
    inv_item = lax.rsqrt(jnp.maximum(deg_item, 1).astype(jnp.float32))
    return ((inv_user[:, None] * mask_blk.astype(jnp.float32)) * inv_item[None, :]).astype(jnp.bfloat16)


def solution(mesh):
    n_col = mesh.shape["col"]
    n_row = mesh.shape["row"]

    def local_fn(mask_blk, user_sh, item_sh, triples):
        adj_blk = norm_adjacency(mask_blk)
        user_cur = user_sh
        item_cur = item_sh
        user_acc = user_sh.astype(jnp.float32)
        item_acc = item_sh.astype(jnp.float32)
        for layer_idx in range(NUM_LAYERS):
            item_panel = lax.all_gather(item_cur, "row", axis=0, tiled=True)
            user_part = jnp.dot(adj_blk, item_panel, preferred_element_type=jnp.float32)
            user_next = lax.psum_scatter(user_part, "col", scatter_dimension=0, tiled=True).astype(jnp.bfloat16)
            user_panel = lax.all_gather(user_cur, "col", axis=0, tiled=True)
            item_part = lax.dot_general(adj_blk, user_panel, (((0,), (0,)), ((), ())), preferred_element_type=jnp.float32)
            item_next = lax.psum_scatter(item_part, "row", scatter_dimension=0, tiled=True).astype(jnp.bfloat16)
            user_acc = user_acc + user_next.astype(jnp.float32)
            item_acc = item_acc + item_next.astype(jnp.float32)
            user_cur = user_next
            item_cur = item_next
        final_user = (user_acc / (NUM_LAYERS + 1)).astype(jnp.bfloat16)
        final_item = (item_acc / (NUM_LAYERS + 1)).astype(jnp.bfloat16)
        user_off = (lax.axis_index("row") * n_col + lax.axis_index("col")) * final_user.shape[0]
        item_off = (lax.axis_index("col") * n_row + lax.axis_index("row")) * final_item.shape[0]
        return final_user, final_item, bpr_terms(final_user, final_item, triples, user_off, item_off)

    return jax.shard_map(
        local_fn, mesh=mesh,
        in_specs=(P("row", "col"), P(("row", "col"), "emb"), P(("col", "row"), "emb"), P()),
        out_specs=(P(("row", "col"), "emb"), P(("col", "row"), "emb"), P()),
        check_vma=False)
```

profile of v0, /device:TPU:1, one launch (start us, length us, event | category | flops | bytes accessed | tf_op | source)
XLA Modules:
  0.0 457.9 jit_solution(8489547203571722368)
XLA Ops:
  7.2 9.2 %fusion.4 = (s32[256]{0:T(256)S(1)}, s32[16384]{0:T(1024)}) fusion(s32[256,16384]{1,0:T(8,128)} %param.6), kind=kLoop, calls=%fused_computation.35 | loop fusion | flops 8371968 | bytes 16843776 | tf_op jit(solution)/shard_map/reduce_sum | solution.py:32
  16.5 7.9 %psum.28 = s32[256]{0:T(256)S(1)} all-reduce(s32[256]{0:T(256)S(1)} %get-tuple-element.7), channel_id=1, replica_groups=mesh['emb'=4,'col'=4,'row'=8] {'col'}, use_global_device_ids=true, to_apply=%region_1.0 | all-reduce | flops 256 | bytes 2048 | tf_op jit(solution)/shard_map/psum | solution.py:32
  24.4 16.0 %all_gather.18 = bf16[16384,16]{0,1:T(8,128)(2,1)S(1)} all-gather(bf16[2048,16]{0,1:T(8,128)(2,1)S(1)} %copy-done.2), channel_id=1, replica_groups=mesh['emb'=4,'col'=4,'row'=8] {'row'}, dimensions={0}, use_global_device_ids=true | all-gather | bytes 589824 | tf_op jit(solution)/shard_map/all_gather | solution.py:50
  40.4 8.9 %all-gather = bf16[4,64,16]{1,2,0:T(8,128)(2,1)S(1)} all-gather(bf16[1,64,16]{1,2,0:T(8,128)(2,1)S(1)} %bitcast.38), channel_id=1, replica_groups=mesh['emb'=4,'col'=4,'row'=8] {'col'}, dimensions={0}, use_global_device_ids=true | all-gather | bytes 10240 | tf_op jit(solution)/shard_map/all_gather | solution.py:53
  49.5 27.8 %all-reduce.3.cloned.1.call-done = s32[16384]{0:T(1024)} async-done(((s32[16384]{0:T(1024)}), s32[16384]{0:T(1024)}) %all-reduce.3.cloned.1.call-update) | async-done | bytes 65552 | tf_op jit(solution)/shard_map/psum | solution.py:33
  78.1 7.1 %multiply_convert_fusion = bf16[256,16384]{1,0:T(8,128)(2,1)S(1)} fusion(s32[256,16384]{1,0:T(8,128)} %param.6, f32[16384]{0:T(1024)S(1)} %convert_rsqrt_fusion, f32[256]{0:T(256)S(1)} %convert_rsqrt_fusion.1), kind=kLoop, calls=%fused_computation.3 | loop fusion | flops 16777216 | bytes 25232384 | tf_op jit(solution)/shard_map/convert_element_type | solution.py:36
  85.2 3.2 copy-done
  88.4 3.0 fusion.5
  91.4 5.7 %fusion.8 = f32[16384,16]{0,1:T(8,128)} fusion(bf16[256,16]{0,1:T(8,128)(2,1)S(1)} %reshape.54, bf16[256,16384]{1,0:T(8,128)(2,1)} %copy-done), kind=kOutput, calls=%fused_computation.39 | convolution fusion | flops 134217728 | bytes 9445376 | tf_op jit(solution)/shard_map/dot_general | solution.py:54
  97.2 13.9 %reduce-scatter.19.cloned.1.call-done = f32[64,16]{1,0:T(8,128)} async-done(((f32[256,16]{1,0:T(8,128)}), f32[64,16]{1,0:T(8,128)}) %reduce-scatter.19.cloned.1.call-update) | async-done | bytes 4112
  112.0 8.9 %all-gather.1 = bf16[4,64,16]{1,2,0:T(8,128)(2,1)S(1)} all-gather(bf16[1,64,16]{1,2,0:T(8,128)(2,1)S(1)} %bitcast.36), channel_id=1, replica_groups=mesh['emb'=4,'col'=4,'row'=8] {'col'}, dimensions={0}, use_global_device_ids=true | all-gather | bytes 10240 | tf_op jit(solution)/shard_map/all_gather | solution.py:53
  121.0 24.1 %reduce-scatter.13.cloned.1.call-done = f32[2048,16]{0,1:T(8,128)} async-done(((f32[16384,16]{0,1:T(8,128)}), f32[2048,16]{0,1:T(8,128)}) %reduce-scatter.13.cloned.1.call-update) | async-done | bytes 131088 | tf_op jit(solution)/shard_map/reduce_scatter | solution.py:55
  146.0 16.2 %all_gather.20 = bf16[16384,16]{0,1:T(8,128)(2,1)S(1)} all-gather(bf16[2048,16]{0,1:T(8,128)(2,1)S(1)} %convert_element_type.76), channel_id=1, replica_groups=mesh['emb'=4,'col'=4,'row'=8] {'row'}, dimensions={0}, use_global_device_ids=true | all-gather | bytes 589824 | tf_op jit(solution)/shard_map/all_gather | solution.py:50
  162.2 6.4 %fusion.6 = f32[256,16]{1,0:T(8,128)} fusion(bf16[256,16384]{1,0:T(8,128)(2,1)} %copy-done, bf16[16384,16]{0,1:T(8,128)(2,1)S(1)} %all_gather.20), kind=kOutput, calls=%fused_computation.37 | convolution fusion | flops 134217728 | bytes 8929280
  168.9 5.7 %fusion.9 = f32[16384,16]{0,1:T(8,128)} fusion(bf16[256,16]{0,1:T(8,128)(2,1)S(1)} %reshape.56, bf16[256,16384]{1,0:T(8,128)(2,1)} %copy-done), kind=kOutput, calls=%fused_computation.40 | convolution fusion | flops 134217728 | bytes 9445376 | tf_op jit(solution)/shard_map/dot_general | solution.py:54
  174.6 11.8 %reduce-scatter.21.cloned.1.call-done = f32[64,16]{1,0:T(8,128)} async-done(((f32[256,16]{1,0:T(8,128)}), f32[64,16]{1,0:T(8,128)}) %reduce-scatter.21.cloned.1.call-update) | async-done | bytes 4112
  187.2 8.9 %all-gather.2 = bf16[4,64,16]{1,2,0:T(8,128)(2,1)S(1)} all-gather(bf16[1,64,16]{1,2,0:T(8,128)(2,1)S(1)} %bitcast.37), channel_id=1, replica_groups=mesh['emb'=4,'col'=4,'row'=8] {'col'}, dimensions={0}, use_global_device_ids=true | all-gather | bytes 10240 | tf_op jit(solution)/shard_map/all_gather | solution.py:53
  196.3 5.6 %fusion.10 = f32[16384,16]{0,1:T(8,128)} fusion(bf16[256,16]{0,1:T(8,128)(2,1)S(1)} %reshape.58, bf16[256,16384]{1,0:T(8,128)(2,1)} %copy-done), kind=kOutput, calls=%fused_computation.41 | convolution fusion | flops 134217728 | bytes 9445376 | tf_op jit(solution)/shard_map/dot_general | solution.py:54
  202.3 17.9 %reduce-scatter.15.cloned.1.call-done = f32[2048,16]{0,1:T(8,128)} async-done(((f32[16384,16]{0,1:T(8,128)}), f32[2048,16]{0,1:T(8,128)}) %reduce-scatter.15.cloned.1.call-update) | async-done | bytes 131088 | tf_op jit(solution)/shard_map/reduce_scatter | solution.py:55
  220.2 33.2 %reduce-scatter.17.cloned.1.call-done = f32[2048,16]{0,1:T(8,128)} async-done(((f32[16384,16]{0,1:T(8,128)}), f32[2048,16]{0,1:T(8,128)}) %reduce-scatter.17.cloned.1.call-update) | async-done | bytes 131088 | tf_op jit(solution)/shard_map/reduce_scatter | solution.py:55
  254.5 16.2 %all_gather.22 = bf16[16384,16]{0,1:T(8,128)(2,1)S(1)} all-gather(bf16[2048,16]{0,1:T(8,128)(2,1)S(1)} %get-tuple-element.15), channel_id=1, replica_groups=mesh['emb'=4,'col'=4,'row'=8] {'row'}, dimensions={0}, use_global_device_ids=true | all-gather | bytes 589824 | tf_op jit(solution)/shard_map/all_gather | solution.py:50
  270.7 6.4 %fusion.7 = f32[256,16]{1,0:T(8,128)} fusion(bf16[256,16384]{1,0:T(8,128)(2,1)} %copy-done, bf16[16384,16]{0,1:T(8,128)(2,1)S(1)} %all_gather.22), kind=kOutput, calls=%fused_computation.38 | convolution fusion | flops 134217728 | bytes 8929280
  277.4 12.1 %gather_fusion.2 = bf16[4096,16]{1,0:T(8,128)(2,1)S(1)} fusion(bf16[2048,16]{1,0:T(8,128)(2,1)S(1)} %copy.35, s32[4096]{0:T(1024)S(1)} %fusion.3), kind=kCustom, calls=%fused_computation.1.clone | custom fusion | bytes 278528 | tf_op jit(solution)/shard_map/jit(_take)/gather | solution.py:13
  289.6 14.9 %gather_fusion.1 = bf16[4096,16]{1,0:T(8,128)(2,1)} fusion(bf16[2048,16]{1,0:T(8,128)(2,1)S(1)} %copy.35, s32[4096]{0:T(1024)S(1)} %fusion.2), kind=kCustom, calls=%fused_computation.clone | custom fusion | bytes 278528 | tf_op jit(solution)/shard_map/jit(_take)/gather | solution.py:13
  304.5 7.0 %convert_select_fusion = (f32[4096,16]{1,0:T(8,128)}, f32[4096,16]{1,0:T(8,128)S(1)}) fusion(bf16[4096,16]{1,0:T(8,128)(2,1)S(1)} %gather_fusion.2, pred[4096]{0:T(1024)(128)(4,1)S(1)} %compare_and_fusion, pred[4096]{0:T(1024)(128)(4,1)S(1)} %get-tuple-element.17, bf16[4096,16]{1,0:T(8,128)(2,1)} %gather_fusion.1, pred[4096]{0:T(1024)(128)(4,1)S(1)} %compare_and_fusion.1, ...), kind=kLoop, calls=%fused_computation.4 | loop fusion | flops 393216 | bytes 802816 | tf_op jit(solution)/shard_map/jit(_where)/select_n | solution.py:14
  311.5 2.2 copy.39
  313.6 1.3 copy.38
  315.9 12.1 %gather_fusion = bf16[4096,16]{1,0:T(8,128)(2,1)S(1)} fusion(bf16[64,16]{1,0:T(8,128)(2,1)S(1)} %copy.34, s32[4096]{0:T(1024)S(1)} %broadcast_clamp_fusion), kind=kCustom, calls=%fused_computation.2 | custom fusion | bytes 278528 | tf_op jit(solution)/shard_map/jit(_take)/gather | solution.py:13
  328.0 1.3 convert_select_fusion.2
  329.9 1.9 pad_maximum_fusion
  331.8 104.1 %all-reduce.5.cloned.1.call-done = f32[12288,16]{0,1:T(8,128)} async-done(((f32[12288,16]{0,1:T(8,128)}), f32[12288,16]{0,1:T(8,128)}) %all-reduce.5.cloned.1.call-update) | async-done | bytes 786448 | tf_op jit(solution)/shard_map/psum | solution.py:23
  437.1 13.3 %psum.31 = f32[4096]{0:T(1024)S(1)} all-reduce(f32[4096]{0:T(1024)S(1)} %fusion.1), channel_id=1, replica_groups=mesh['emb'=4,'col'=4,'row'=8] {'emb'}, use_global_device_ids=true, to_apply=%region_12.14 | all-reduce | flops 4096 | bytes 32768 | tf_op jit(solution)/shard_map/psum | solution.py:27
  (56 shorter events, 9.3 us)
Async XLA Ops:
  7.2 17.3 %copy-start.2 = (bf16[2048,16]{0,1:T(8,128)(2,1)S(1)}, bf16[2048,16]{0,1:T(8,128)(2,1)}, u32[]{:S(2)}) copy-start(bf16[2048,16]{0,1:T(8,128)(2,1)} %param.8) | copy-start | bytes 196612
  7.2 33.3 %copy-start.5 = (bf16[64,16]{0,1:T(8,128)(2,1)S(1)}, bf16[64,16]{0,1:T(8,128)(2,1)}, u32[]{:S(2)}) copy-start(bf16[64,16]{0,1:T(8,128)(2,1)} %param.7) | copy-start | bytes 6148
  7.2 70.0 %all-reduce.3.cloned.1.call-start = ((), (), s32[]{:S(2)}) async-start(), calls=%async_computation.6 | async-start | bytes 131072 | tf_op jit(solution)/shard_map/psum | solution.py:33
  16.5 94.6 %reduce-scatter.19.cloned.1.call-start = ((), (), s32[]{:S(2)}) async-start(), calls=%async_computation.11 | async-start | bytes 163840
  85.2 3.2 copy-start
  91.4 53.7 %reduce-scatter.13.cloned.1.call-start = ((), (), s32[]{:S(2)}) async-start(), calls=%async_computation.7 | async-start | bytes 1179648 | tf_op jit(solution)/shard_map/reduce_scatter | solution.py:55
  97.1 89.3 %reduce-scatter.21.cloned.1.call-start = ((), (), s32[]{:S(2)}) async-start(), calls=%async_computation.12 | async-start | bytes 163840
  168.6 33.3 %copy-start.4 = (s32[4096,3]{0,1:T(4,128)S(1)}, s32[4096,3]{0,1:T(4,128)}, u32[]{:S(2)}) copy-start(s32[4096,3]{0,1:T(4,128)} %param.9) | copy-start | bytes 147460
  168.6 84.8 %copy-start.1 = (f32[2048,16]{0,1:T(8,128)S(1)}, f32[2048,16]{0,1:T(8,128)}, u32[]{:S(2)}) copy-start(f32[2048,16]{0,1:T(8,128)} %reduce-scatter.13.cloned.1.call-done) | copy-start | bytes 393220
  168.7 51.6 %reduce-scatter.15.cloned.1.call-start = ((), (), s32[]{:S(2)}) async-start(), calls=%async_computation.8 | async-start | bytes 1179648 | tf_op jit(solution)/shard_map/reduce_scatter | solution.py:55
  174.6 78.9 %reduce-scatter.17.cloned.1.call-start = ((), (), s32[]{:S(2)}) async-start(), calls=%async_computation.9 | async-start | bytes 1179648 | tf_op jit(solution)/shard_map/reduce_scatter | solution.py:55
  201.8 113.1 %reduce-scatter.23.cloned.1.call-start = ((), (), s32[]{:S(2)}) async-start(), calls=%async_computation.13 | async-start | bytes 163840
  254.5 35.1 %copy-start.3 = (bf16[2048,16]{0,1:T(8,128)(2,1)}, bf16[2048,16]{0,1:T(8,128)(2,1)S(1)}, u32[]{:S(2)}) copy-start(bf16[2048,16]{0,1:T(8,128)(2,1)S(1)} %get-tuple-element.14) | copy-start | bytes 196612
  277.1 158.8 %all-reduce.5.cloned.1.call-start = ((), (), s32[]{:S(2)}) async-start(), calls=%async_computation.10 | async-start | bytes 1572864 | tf_op jit(solution)/shard_map/psum | solution.py:23
  315.8 16.0 %copy-start.6 = (bf16[64,16]{0,1:T(8,128)(2,1)}, bf16[64,16]{0,1:T(8,128)(2,1)S(1)}, u32[]{:S(2)}) copy-start(bf16[64,16]{0,1:T(8,128)(2,1)S(1)} %multiply_convert_fusion.2) | copy-start | bytes 6148
Sparse Core Ops, SparseCore 0:
  16.6 60.5 all-reduce.2
  91.5 19.5 reduce-scatter.18
  113.5 31.5 reduce-scatter.12
  168.8 17.6 reduce-scatter.20
  188.6 31.5 reduce-scatter.14
  222.5 30.9 reduce-scatter.16
  277.2 17.6 reduce-scatter.22
  331.9 103.9 all-reduce.4
where the time goes:
time: 462 us; the launch traced here: 458 us
  waiting for transfers between devices  233 us (50%)
  blocking collectives  96.5 us (21%)
  local copies, waits for them, and re-layouts  49.6 us (11%)
  matrix products  32.6 us (7%)
  other arithmetic  31.4 us (7%)
  between operations  14.4 us (3%)
    psum x1, waiting for transfers between devices, bpr_terms(): fetched = lax.psum(fetched, ('row', 'col'))  104 us
    reduce_scatter x3, waiting for transfers between devices, local_fn(): lax.psum_scatter(item_part, 'row', scatter_dimension=0, tiled=True)  75.2 us
    all_gather x3, blocking collectives, local_fn(): item_panel = lax.all_gather(item_cur, 'row', axis=0, tiled=True)  48.5 us
    gather x3, local copies, waits for them, and re-layouts, lookup_rows(): picked = jnp.take(table, jnp.clip(local_ids, 0, own_rows - 1), axis=0)  39.2 us
    psum x1, waiting for transfers between devices, norm_adjacency(): deg_item = lax.psum(jnp.sum(mask_blk, axis=0), 'row')  27.8 us
    all_gather x3, blocking collectives, local_fn(): user_panel = lax.all_gather(user_cur, 'col', axis=0, tiled=True)  26.8 us
    unnamed x11, waiting for transfers between devices  25.9 us
    dot_general x3, matrix products, local_fn(): lax.dot_general(adj_blk, user_panel, (((0,), (0,)), ((), ())), preferred_...  16.9 us
  transfers between devices with their start and end apart: 8, of which 7 were waited for; matrix products, arithmetic and copies ran while one was open for 12% of the time, Pallas kernels for 0%

commit v1 on v0

v1 whole, which is shorter than its diff:
```python
import jax
import jax.numpy as jnp
from jax import lax
from jax.experimental import pallas as pl
from jax.experimental.pallas import tpu as pltpu
from jax.sharding import PartitionSpec as P

NUM_LAYERS = 3
MESH = pl.DeviceIdType.MESH
F32 = jnp.float32
BF16 = jnp.bfloat16
EMB = 64
COLS = 16
LANE = 128
CHUNK = 512
ITEMS = 2048
USERS = 256
PEERS = 32
OTHERS = PEERS - 1


def pack_half(top, bot, lane_lo):
    first = jnp.where(lane_lo, top, pltpu.roll(bot, EMB, 1))
    second = jnp.where(lane_lo, pltpu.roll(top, EMB, 1), bot)
    return first, second


def unpack_half(first, second, lane_lo):
    top = jnp.where(lane_lo, first, pltpu.roll(second, EMB, 1))
    bot = jnp.where(lane_lo, pltpu.roll(first, EMB, 1), second)
    return top, bot


def pick_rows(table, ids):
    n = ids.shape[1]
    low = jnp.bitwise_and(ids, 127)
    high = lax.shift_right_arithmetic(ids, 7)
    hot = (lax.broadcasted_iota(jnp.int32, (LANE, n), 0) == low).astype(F32).astype(BF16)
    wide = jnp.dot(table, hot, preferred_element_type=F32)
    high16 = jnp.broadcast_to(high, (COLS, n))
    total = jnp.zeros((COLS, n), F32)
    for blk in range(COLS):
        total = total + jnp.where(high16 == blk, wide[blk * COLS:(blk + 1) * COLS], 0.0)
    return total


def place():
    e = lax.axis_index("emb")
    c = lax.axis_index("col")
    r = lax.axis_index("row")
    return e, c, r, r // 2, r % 2


def device(r, c, e):
    return (e, c, r)


def loop(n, body):
    lax.fori_loop(1, n, lambda j, carry: (body(j), carry)[1], 0)


class Links:
    def __init__(self, send_sem, recv_sem):
        self.send_sem = send_sem
        self.recv_sem = recv_sem

    def send(self, src, dst, phase, target):
        pltpu.make_async_remote_copy(src_ref=src, dst_ref=dst, send_sem=self.send_sem.at[phase],
                                     recv_sem=self.recv_sem.at[phase], device_id=target, device_id_type=MESH).start()

    def wait_recv(self, ref, phase):
        pltpu.make_async_copy(ref, ref, self.recv_sem.at[phase]).wait()

    def wait_send(self, ref, phase):
        pltpu.make_async_copy(ref, ref, self.send_sem.at[phase]).wait()


def greet(target):
    pl.semaphore_signal(pltpu.get_barrier_semaphore(), inc=1, device_id=target, device_id_type=MESH)


def load_kernel(mask_ref, own_ref, other_ref, du_ref, di_ref, m_loc, sems):
    e, c, r, x, k = place()
    loads = []
    for par in (1, 0):
        for xx in range(4):
            row = 2 * xx + jnp.bitwise_xor(k, par)
            off = pl.multiple_of(row * ITEMS + e * CHUNK, CHUNK)
            cp = pltpu.make_async_copy(mask_ref.at[:, pl.ds(off, CHUNK)], m_loc.at[par, xx], sems.at[par * 4 + xx])
            cp.start()
            loads.append((par, xx, cp))
    lanes = jnp.zeros((USERS, LANE), F32)
    for par, xx, cp in loads:
        cp.wait()
        m = m_loc[par, xx].astype(F32)
        (other_ref if par else own_ref)[xx] = m.astype(BF16)
        di_ref[par, :, xx * CHUNK:(xx + 1) * CHUNK] = jnp.sum(m, axis=0, keepdims=True)
        for g in range(4):
            lanes = lanes + m[:, g * LANE:(g + 1) * LANE]
    rows = lax.dot_general(jnp.ones((8, LANE), BF16), lanes.astype(BF16), (((1,), (1,)), ((), ())),
                           preferred_element_type=F32)
    du_ref[...] = rows[0:1]


def degree_kernel(other_ref, du_ref, di_ref, rem_ref, su_ref, si_ref, du, di, send_sem, recv_sem):
    e, c, r, x, k = place()
    q = k * COLS + c * 4 + e
    links = Links(send_sem, recv_sem)

    def q_dev(qq):
        return device(2 * x + qq // COLS, (qq // 4) % 4, qq % 4)

    loop(PEERS, lambda j: greet(q_dev(lax.rem(q + j, PEERS))))
    for j in range(2, 8):
        greet(device(2 * lax.rem(x + j // 2, 4) + j % 2, c, e))
    pl.semaphore_wait(pltpu.get_barrier_semaphore(), OTHERS + 6)
    loop(PEERS, lambda j: links.send(du_ref, du.at[q], 0, q_dev(lax.rem(q + j, PEERS))))
    for j in range(1, 8):
        links.send(di_ref.at[j % 2], di.at[r], 1, device(lax.rem(r + j, 8), c, e))
    links.send(other_ref, rem_ref, 2, device(2 * x + 1 - k, c, e))
    du[q] = du_ref[...]
    di[r] = di_ref[0]
    links.wait_recv(du.at[pl.ds(0, OTHERS)], 0)
    for half in range(2):
        su_ref[half] = jnp.sum(du[half * COLS:(half + 1) * COLS], axis=0)
    links.wait_recv(di.at[pl.ds(0, 7)], 1)
    si_ref[...] = jnp.sum(di[...], axis=0)
    links.wait_recv(rem_ref, 2)
    links.wait_send(du.at[pl.ds(0, OTHERS)], 0)
    links.wait_send(di.at[pl.ds(0, 7)], 1)
    links.wait_send(rem_ref, 2)


def build_kernel(own_ref, rem_ref, su_ref, si_ref, adj_ref):
    k = lax.axis_index("row") % 2
    inv_i = lax.rsqrt(jnp.maximum(si_ref[...], 1.0))
    for source, half in ((own_ref, k), (rem_ref, 1 - k)):
        inv_u = lax.rsqrt(jnp.maximum(su_ref[half], 1.0))
        for rc in range(2):
            col = jnp.broadcast_to(inv_u[:, rc * LANE:(rc + 1) * LANE], (LANE, LANE)).T
            base = pl.multiple_of(half * USERS + rc * LANE, LANE)
            for xx in range(4):
                m = source[xx, rc * LANE:(rc + 1) * LANE, :].astype(F32)
                for g in range(4):
                    lo = xx * CHUNK + g * LANE
                    val = (col * m[:, g * LANE:(g + 1) * LANE]) * inv_i[:, lo:lo + LANE]
                    adj_ref[pl.ds(base, LANE), lo:lo + LANE] = val.astype(BF16)


S_FIN = 0
S_UAG = 1
S_IAG = S_UAG + NUM_LAYERS
S_URS = S_IAG + NUM_LAYERS
S_IRS = S_URS + NUM_LAYERS
N_SEM = S_IRS + NUM_LAYERS


def layers_kernel(adj, ut_v, it_v, ou_ref, oi_ref, pu_ref, uag, iag, usend, urecv, isend, irecv, utp, ei, fin,
                  acc_i, send_sem, recv_sem):
    e, c, r, x, k = place()
    q = k * COLS + c * 4 + e
    links = Links(send_sem, recv_sem)
    send, wait_recv, wait_send = links.send, links.wait_recv, links.wait_send

    def q_dev(qq):
        return device(2 * x + qq // COLS, (qq // 4) % 4, qq % 4)

    def xz_dev(idx):
        return device(2 * (idx // 4) + k, c, idx % 4)

    loop(PEERS, lambda j: greet(q_dev(lax.rem(q + j, PEERS))))
    for j in range(1, 4):
        for dz in range(4):
            greet(device(2 * lax.rem(x + j, 4) + k, c, lax.rem(e + dz, 4)))
    pl.semaphore_wait(pltpu.get_barrier_semaphore(), OTHERS + 12)

    lane_lo = lax.broadcasted_iota(jnp.int32, (8, LANE), 1) < EMB

    def send_uag(layer):
        loop(PEERS, lambda j: send(uag.at[layer, q], uag.at[layer, q], S_UAG + layer, q_dev(lax.rem(q + j, PEERS))))

    def send_iag(layer):
        slot = layer % 2
        for j in (2, 1, 3):
            mine = iag.at[slot, pl.ds(x * 4, 4)]
            send(mine, mine, S_IAG + layer, device(2 * lax.rem(x + j, 4) + k, c, e))

    user0 = ut_v[...].astype(F32)
    packed = jnp.concatenate([user0[0:8], user0[8:COLS]], axis=1)
    uag[0, q] = packed.astype(BF16)
    acc_u = packed
    send_uag(0)
    iag[0, x * 4 + e] = it_v[:, pl.ds(pl.multiple_of(e * CHUNK, CHUNK), CHUNK)]

    def send_i0(j):
        idx = lax.rem(x * 4 + e + j, COLS)
        send(it_v.at[:, pl.ds(pl.multiple_of((idx % 4) * CHUNK, CHUNK), CHUNK)],
             iag.at[0, x * 4 + e], S_IAG, xz_dev(idx))

    loop(COLS, send_i0)

    for layer in range(NUM_LAYERS):
        slot = layer % 2
        wait_recv(uag.at[layer, pl.ds(0, OTHERS)], S_UAG + layer)
        for g in range(4):
            for ee in range(4):
                s0 = (g // 2) * COLS + (g % 2) * 8 + ee
                top, bot = unpack_half(uag[layer, s0].astype(F32), uag[layer, s0 + 4].astype(F32), lane_lo)
                utp[ee * COLS:(ee + 1) * COLS, g * LANE:(g + 1) * LANE] = jnp.concatenate([top, bot], axis=0).astype(BF16)
        if layer >= 2:
            wait_send(irecv.at[0, pl.ds(0, 3)], S_IRS + layer - 2)
        for j in (2, 1, 3, 0):
            xx = lax.rem(x + j, 4)
            part = jnp.dot(utp[...], adj[:, pl.ds(pl.multiple_of(xx * CHUNK, CHUNK), CHUNK)], preferred_element_type=F32)
            if j == 0:
                irecv[slot, x] = part
            else:
                isend[slot, j - 1] = part
                send(isend.at[slot, j - 1], irecv.at[slot, x], S_IRS + layer, device(2 * xx + k, c, e))
        if layer == 0:
            wait_recv(iag.at[0, pl.ds(0, 15)], S_IAG)
        else:
            wait_recv(iag.at[slot, pl.ds(0, 12)], S_IAG + layer)
        part = jnp.zeros((EMB, CHUNK), F32)
        for xx in range(4):
            part = part + lax.dot_general(iag[slot, xx * 4:(xx + 1) * 4].reshape(EMB, CHUNK), adj[:, xx * CHUNK:(xx + 1) * CHUNK], (((1,), (1,)), ((), ())),
                                          preferred_element_type=F32)
        if layer == 0:
            acc_i[...] = iag[0, pl.ds(x * 4, 4)].reshape(EMB, CHUNK).astype(F32)
        if layer >= 1:
            wait_send(urecv.at[pl.ds(0, OTHERS)], S_URS + layer - 1)
        for g in range(4):
            for ee in range(4):
                s0 = (g // 2) * COLS + (g % 2) * 8 + ee
                v = part[ee * COLS:(ee + 1) * COLS, g * LANE:(g + 1) * LANE]
                first, second = pack_half(v[0:8], v[8:COLS], lane_lo)
                usend[s0] = first
                usend[s0 + 4] = second

        def send_u(j, layer=layer):
            qq = lax.rem(q + j, PEERS)
            send(usend.at[qq], urecv.at[q], S_URS + layer, q_dev(qq))

        loop(PEERS, send_u)
        urecv[q] = usend[q]
        wait_recv(urecv.at[pl.ds(0, OTHERS)], S_URS + layer)
        nxt = jnp.sum(urecv[...], axis=0).astype(BF16)
        acc_u = acc_u + nxt.astype(F32)
        if layer + 1 < NUM_LAYERS:
            uag[layer + 1, q] = nxt
            send_uag(layer + 1)
        wait_recv(irecv.at[slot, pl.ds(0, 3)], S_IRS + layer)
        nxt = ((irecv[slot, 0] + irecv[slot, 1]) + (irecv[slot, 2] + irecv[slot, 3])).astype(BF16)
        if layer + 1 < NUM_LAYERS:
            iag[(layer + 1) % 2, pl.ds(x * 4, 4)] = nxt.reshape(4, COLS, CHUNK)
            send_iag(layer + 1)
        acc_i[...] = acc_i[...] + nxt.astype(F32)

    ei[...] = (acc_i[...] / (NUM_LAYERS + 1)).astype(BF16)
    fin[e] = ei[pl.ds(pl.multiple_of(e * COLS, COLS), COLS), :]
    for j in range(1, 4):
        ee = lax.rem(e + j, 4)
        send(ei.at[pl.ds(pl.multiple_of(ee * COLS, COLS), COLS), :], fin.at[e], S_FIN, device(r, c, ee))
    fin_u = (acc_u / (NUM_LAYERS + 1)).astype(BF16)
    pu_ref[...] = fin_u
    fin_u = fin_u.astype(F32)
    ou_ref[...] = jnp.concatenate([fin_u[:, 0:EMB], pltpu.roll(fin_u, EMB, 1)[:, 0:EMB]], axis=0).astype(BF16)
    for layer in range(NUM_LAYERS):
        wait_send(uag.at[layer, pl.ds(0, OTHERS)], S_UAG + layer)
        if layer == 0:
            wait_send(iag.at[0, pl.ds(0, 15)], S_IAG)
        else:
            wait_send(iag.at[layer % 2, pl.ds(0, 12)], S_IAG + layer)
    wait_send(urecv.at[pl.ds(0, OTHERS)], S_URS + NUM_LAYERS - 1)
    wait_send(irecv.at[0, pl.ds(0, 3)], S_IRS + NUM_LAYERS - 2)
    wait_send(irecv.at[0, pl.ds(0, 3)], S_IRS + NUM_LAYERS - 1)
    wait_send(fin.at[pl.ds(0, 3)], S_FIN)
    wait_recv(fin.at[pl.ds(0, 3)], S_FIN)
    for s in range(4):
        oi_ref[:, s * CHUNK:(s + 1) * CHUNK] = fin[s]


def loss_kernel(pu_ref, it_ref, tr_ref, ol_ref, eu, wmat, umat, dsend, drecv, sz, lag, send_sem, recv_sem):
    e, c, r, x, k = place()
    b = r * 4 + c
    links = Links(send_sem, recv_sem)
    send, wait_recv, wait_send = links.send, links.wait_recv, links.wait_send

    def b_dev(bb):
        return device(bb // 4, bb % 4, e)

    loop(PEERS, lambda j: greet(b_dev(lax.rem(b + j, PEERS))))
    for j in range(1, 4):
        greet(device(r, c, lax.rem(e + j, 4)))
    lane_lo = lax.broadcasted_iota(jnp.int32, (8, LANE), 1) < EMB
    for h in range(COLS):
        wmat[h * COLS:(h + 1) * COLS, :] = it_ref[:, h * LANE:(h + 1) * LANE]
    eu[b] = pu_ref[...]
    first_item = (c * 8 + r) * ITEMS

    def differences(t, carry):
        ids = tr_ref[:, pl.ds(pl.multiple_of(t * CHUNK, CHUNK), CHUNK)] - first_item
        diff = pick_rows(wmat[...], ids[1:2]) - pick_rows(wmat[...], ids[2:3])
        for g in range(4):
            dsend[t * 4 + g] = diff[:, g * LANE:(g + 1) * LANE]
        return carry

    lax.fori_loop(0, 8, differences, 0)
    pl.semaphore_wait(pltpu.get_barrier_semaphore(), OTHERS + 3)
    loop(PEERS, lambda j: send(eu.at[b], eu.at[b], 0, b_dev(lax.rem(b + j, PEERS))))

    def send_d(j):
        bb = lax.rem(b + j, PEERS)
        send(dsend.at[bb], drecv.at[b], 1, b_dev(bb))

    loop(PEERS, send_d)
    drecv[b] = dsend[b]
    wait_recv(eu.at[pl.ds(0, OTHERS)], 0)
    for g in range(COLS):
        top, bot = unpack_half(eu[2 * g].astype(F32), eu[2 * g + 1].astype(F32), lane_lo)
        umat[g * COLS:(g + 1) * COLS, :] = jnp.concatenate([top, bot], axis=0).astype(BF16)
    e_user = pick_rows(umat[...], tr_ref[0:1, pl.ds(pl.multiple_of(b * LANE, LANE), LANE)])
    wait_recv(drecv.at[pl.ds(0, OTHERS)], 1)
    sz[e] = jnp.sum(e_user * jnp.sum(drecv[...], axis=0), axis=0, keepdims=True)
    for j in range(1, 4):
        send(sz.at[e], sz.at[e], 2, device(r, c, lax.rem(e + j, 4)))
    wait_recv(sz.at[pl.ds(0, 3)], 2)
    score = (sz[0] + sz[1]) + (sz[2] + sz[3])
    lag[b] = jnp.maximum(-score, 0.0) + jnp.log1p(jnp.exp(-jnp.abs(score)))
    loop(PEERS, lambda j: send(lag.at[b], lag.at[b], 3, b_dev(lax.rem(b + j, PEERS))))
    wait_send(eu.at[pl.ds(0, OTHERS)], 0)
    wait_send(drecv.at[pl.ds(0, OTHERS)], 1)
    wait_send(sz.at[pl.ds(0, 3)], 2)
    wait_recv(lag.at[pl.ds(0, OTHERS)], 3)
    wait_send(lag.at[pl.ds(0, OTHERS)], 3)
    for s in range(PEERS):
        ol_ref[s:s + 1, :] = lag[s]


def call(body, outs, in_specs, scratch, collective_id=None, vmem_mib=24):
    vmem = pl.BlockSpec(memory_space=pltpu.VMEM)
    return pl.pallas_call(
        body,
        out_shape=tuple(jax.ShapeDtypeStruct(shape, dtype) for shape, dtype in outs),
        in_specs=[vmem if s is None else s for s in in_specs],
        out_specs=(vmem,) * len(outs),
        scratch_shapes=scratch,
        compiler_params=pltpu.CompilerParams(
            collective_id=collective_id, has_side_effects=collective_id is not None,
            vmem_limit_bytes=vmem_mib * 1024 * 1024),
        name=body.__name__)


def solution(mesh):
    vm = pltpu.VMEM
    dma = pltpu.SemaphoreType.DMA

    def local_fn(mask_blk, user_sh, item_sh, triples):
        half = ((4, USERS, CHUNK), BF16)
        own, other, du, di = call(
            load_kernel, [half, half, ((1, USERS), F32), ((2, 1, ITEMS), F32)], [pl.BlockSpec(memory_space=pl.ANY)],
            [vm((2, 4, USERS, CHUNK), jnp.int32), dma((8,))], vmem_mib=49)(mask_blk)
        rem, su, si = call(
            degree_kernel, [half, ((2, 1, USERS), F32), ((1, ITEMS), F32)], [None] * 3,
            [vm((PEERS, 1, USERS), F32), vm((8, 1, ITEMS), F32), dma((3,)), dma((3,))], 0)(other, du, di)
        adj, = call(build_kernel, [((CHUNK, ITEMS), BF16)], [None] * 4, [])(own, rem, su, si)
        out_u, out_i, packed_u = call(
            layers_kernel, [((COLS, EMB), BF16), ((COLS, ITEMS), BF16), ((8, LANE), BF16)], [None] * 3,
            [vm((NUM_LAYERS, PEERS, 8, LANE), BF16), vm((2, COLS, COLS, CHUNK), BF16), vm((PEERS, 8, LANE), F32),
             vm((PEERS, 8, LANE), F32), vm((2, 3, EMB, CHUNK), F32), vm((2, 4, EMB, CHUNK), F32), vm((EMB, CHUNK), BF16),
             vm((EMB, CHUNK), BF16), vm((4, COLS, CHUNK), BF16), vm((EMB, CHUNK), F32), dma((N_SEM,)), dma((N_SEM,))],
            1)(adj, user_sh.T, item_sh.T)
        loss, = call(
            loss_kernel, [((PEERS, LANE), F32)], [None] * 3,
            [vm((PEERS, 8, LANE), BF16), vm((USERS, LANE), BF16), vm((USERS, LANE), BF16), vm((PEERS, COLS, LANE), F32),
             vm((PEERS, COLS, LANE), F32), vm((4, 1, LANE), F32), vm((PEERS, 1, LANE), F32), dma((4,)), dma((4,))],
            2)(packed_u, out_i, triples.T)
        return out_u.T, out_i.T, loss.reshape(4096)

    return jax.shard_map(
        local_fn, mesh=mesh,
        in_specs=(P("row", "col"), P(("row", "col"), "emb"), P(("col", "row"), "emb"), P()),
        out_specs=(P(("row", "col"), "emb"), P(("col", "row"), "emb"), P()),
        check_vma=False)
```

time: 462 us -> 83.7 us (0.18)
  waiting for transfers between devices: 233 us -> 0 us
  blocking collectives: 96.5 us -> 0 us
  Pallas kernels: 0 us -> 81 us
  local copies, waits for them, and re-layouts: 49.6 us -> 1.84 us
  matrix products: 32.6 us -> 0 us
  other arithmetic: 31.4 us -> 0 us
  between operations: 14.4 us -> 0.72 us
    psum x2 -> x0, waiting for transfers between devices: 132 us -> none  [the longest x1 104 us: bpr_terms(): fetched = lax.psum(fetched, ('row', 'col'))]
    pallas_call x0 -> x5, Pallas kernels: none -> 81 us  [the longest x1 45 us: local_fn(): call(layers_kernel, [((COLS, EMB), BF16), ((COLS, ITEMS), BF16), ((8, LAN...]
    all_gather x6 -> x0, blocking collectives: 75.3 us -> none  [the longest x3 48.5 us: local_fn(): item_panel = lax.all_gather(item_cur, 'row', axis=0, tiled=True)]
    reduce_scatter x3 -> x0, waiting for transfers between devices: 75.2 us -> none  [local_fn(): lax.psum_scatter(item_part, 'row', scatter_dimension=0, tiled=True)]
    gather x3 -> x0, local copies, waits for them, and re-layouts: 39.2 us -> none  [lookup_rows(): picked = jnp.take(table, jnp.clip(local_ids, 0, own_rows - 1), axis=0)]
    unnamed x11 -> x0, waiting for transfers between devices: 25.9 us -> none
    psum x2 -> x0, blocking collectives: 21.2 us -> none  [the longest x1 13.3 us: bpr_terms(): score = lax.psum(jnp.sum(e_user * (e_pos - e_neg), axis=1), 'emb')]
    dot_general x3 -> x0, matrix products: 16.9 us -> none  [local_fn(): lax.dot_general(adj_blk, user_panel, (((0,), (0,)), ((), ())), preferred_...]
  transfers between devices with their start and end apart: 8 -> 0, of which waited for: 7 -> 0; matrix products, arithmetic and copies ran while one was open for 12% -> 0% of each run, Pallas kernels for 0% -> 0%
where the time goes in v1:
time: 83.7 us; the launch traced here: 83.6 us
  Pallas kernels  81 us (97%)
  local copies, waits for them, and re-layouts  1.84 us (2%)
    pallas_call x1, Pallas kernels, local_fn(): call(layers_kernel, [((COLS, EMB), BF16), ((COLS, ITEMS), BF16), ((8, LAN...  45 us
    pallas_call x1, Pallas kernels, local_fn(): call(loss_kernel, [((PEERS, LANE), F32)], [None] * 3, [vm((PEERS, 8, LANE...  19.4 us
    pallas_call x1, Pallas kernels, local_fn(): call(degree_kernel, [half, ((2, 1, USERS), F32), ((1, ITEMS), F32)], [Non...  13.5 us
    pallas_call x1, Pallas kernels, local_fn(): call(load_kernel, [half, half, ((1, USERS), F32), ((2, 1, ITEMS), F32)],...  2.46 us
    unnamed x9, local copies, waits for them, and re-layouts  1.84 us

profile of v1, /device:TPU:1, one launch (start us, length us, event | category | flops | bytes accessed | tf_op | source)
XLA Modules:
  0.0 83.6 jit_solution(6427507323234114291)
XLA Ops:
  0.6 0.0 copy-start.1
  0.6 0.0 copy-start
  0.7 0.0 copy-start.2
  0.7 2.5 %load_kernel.1 = (bf16[4,256,512]{2,1,0:T(8,128)(2,1)S(1)}, bf16[4,256,512]{2,1,0:T(8,128)(2,1)S(1)}, f32[1,256]{1,0:T(1,128)S(1)}, f32[2,1,2048]{2,1,0:T(1,128)S(1)}) custom-call(s32[256,16384]{1,0:T(8,128)} %mask_ref.1), custom_call_target="tpu_custom_call" | custom-call | tf_op jit(solution)/shard_map/load_kernel/pallas_call | solution.py:360
  3.1 13.5 %degree_kernel.1 = (bf16[4,256,512]{2,1,0:T(8,128)(2,1)S(1)}, f32[2,1,256]{2,1,0:T(1,128)S(1)}, f32[1,2048]{1,0:T(1,128)S(1)}) custom-call(bf16[4,256,512]{2,1,0:T(8,128)(2,1)S(1)} %get-tuple-element.14.other_ref, f32[1,256]{1,0:T(1,128)S(1)} %get-tuple-element.15.du_ref, f32[2,1,2048]{2,1,0:T(1,128)S(1)} %get-tuple-element.16.di_ref), custom_call_target="tpu_custom_call" | custom-call | tf_op jit(solution)/shard_map/degree_kernel/pallas_call | solution.py:363
  16.7 0.6 build_kernel.1.adj
  17.3 0.0 copy-done
  17.3 0.0 copy-done.2
  17.3 45.0 %layers_kernel.1 = (bf16[16,64]{1,0:T(8,128)(2,1)S(1)}, bf16[16,2048]{1,0:T(8,128)(2,1)S(1)}, bf16[8,128]{1,0:T(8,128)(2,1)S(1)}) custom-call(bf16[512,2048]{1,0:T(8,128)(2,1)S(1)} %build_kernel.1.adj, bf16[16,64]{1,0:T(8,128)(2,1)S(1)} %bitcast.10, bf16[16,2048]{1,0:T(8,128)(2,1)S(1)} %bitcast.7), custom_call_target="tpu_custom_call" | custom-call | tf_op jit(solution)/shard_map/layers_kernel/pallas_call | solution.py:367
  62.3 0.0 copy-done.1
  62.3 19.4 %loss_kernel.1 = f32[32,128]{1,0:T(8,128)S(1)} custom-call(bf16[8,128]{1,0:T(8,128)(2,1)S(1)} %get-tuple-element.22.pu_ref, bf16[16,2048]{1,0:T(8,128)(2,1)S(1)} %get-tuple-element.21.it_ref, s32[3,4096]{1,0:T(4,128)S(1)} %bitcast.8), custom_call_target="tpu_custom_call" | custom-call | tf_op jit(solution)/shard_map/loss_kernel/pallas_call | solution.py:373
  81.7 0.6 copy.10
  82.3 0.6 copy.11
  83.0 0.6 copy.12
Async XLA Ops:
  0.6 61.7 %copy-start.1 = (s32[4096,3]{0,1:T(4,128)S(1)}, s32[4096,3]{0,1:T(4,128)}, u32[]{:S(2)}) copy-start(s32[4096,3]{0,1:T(4,128)} %param.7) | copy-start | bytes 147460
  0.6 16.7 %copy-start = (bf16[2048,16]{0,1:T(8,128)(2,1)S(1)}, bf16[2048,16]{0,1:T(8,128)(2,1)}, u32[]{:S(2)}) copy-start(bf16[2048,16]{0,1:T(8,128)(2,1)} %param.6) | copy-start | bytes 196612
  0.7 16.7 %copy-start.2 = (bf16[64,16]{0,1:T(8,128)(2,1)S(1)}, bf16[64,16]{0,1:T(8,128)(2,1)}, u32[]{:S(2)}) copy-start(bf16[64,16]{0,1:T(8,128)(2,1)} %param.5) | copy-start | bytes 6148

commit v2 on v0

v2 whole, which is shorter than its diff:
```python
import jax
import jax.numpy as jnp
from jax import lax
from jax.experimental import pallas as pl
from jax.experimental.pallas import tpu as pltpu
from jax.sharding import PartitionSpec as P

NUM_LAYERS = 3
MESH = pl.DeviceIdType.MESH
F32 = jnp.float32
BF16 = jnp.bfloat16
EMB = 64
COLS = 16
LANE = 128
CHUNK = 512
ITEMS = 2048
USERS = 256
PEERS = 32
OTHERS = PEERS - 1


def pack_half(top, bot, lane_lo):
    first = jnp.where(lane_lo, top, pltpu.roll(bot, EMB, 1))
    second = jnp.where(lane_lo, pltpu.roll(top, EMB, 1), bot)
    return first, second


def unpack_half(first, second, lane_lo):
    top = jnp.where(lane_lo, first, pltpu.roll(second, EMB, 1))
    bot = jnp.where(lane_lo, pltpu.roll(first, EMB, 1), second)
    return top, bot


def pick_rows(table, ids):
    n = ids.shape[1]
    low = jnp.bitwise_and(ids, 127)
    high = lax.shift_right_arithmetic(ids, 7)
    hot = (lax.broadcasted_iota(jnp.int32, (LANE, n), 0) == low).astype(F32).astype(BF16)
    wide = jnp.dot(table, hot, preferred_element_type=F32)
    high16 = jnp.broadcast_to(high, (COLS, n))
    total = jnp.zeros((COLS, n), F32)
    for blk in range(COLS):
        total = total + jnp.where(high16 == blk, wide[blk * COLS:(blk + 1) * COLS], 0.0)
    return total


def place():
    e = lax.axis_index("emb")
    c = lax.axis_index("col")
    r = lax.axis_index("row")
    return e, c, r, r // 2, r % 2


def device(r, c, e):
    return (e, c, r)


class Links:
    def __init__(self, send_sem, recv_sem):
        self.send_sem = send_sem
        self.recv_sem = recv_sem

    def send(self, src, dst, phase, target):
        pltpu.make_async_remote_copy(src_ref=src, dst_ref=dst, send_sem=self.send_sem.at[phase],
                                     recv_sem=self.recv_sem.at[phase], device_id=target, device_id_type=MESH).start()

    def wait_recv(self, ref, phase):
        pltpu.make_async_copy(ref, ref, self.recv_sem.at[phase]).wait()

    def wait_send(self, ref, phase):
        pltpu.make_async_copy(ref, ref, self.send_sem.at[phase]).wait()


def greet(target):
    pl.semaphore_signal(pltpu.get_barrier_semaphore(), inc=1, device_id=target, device_id_type=MESH)


def load_kernel(mask_ref, own_ref, other_ref, du_ref, di_ref, m_loc, sems):
    e, c, r, x, k = place()
    loads = []
    for par in (1, 0):
        for xx in range(4):
            row = 2 * xx + jnp.bitwise_xor(k, par)
            off = pl.multiple_of(row * ITEMS + e * CHUNK, CHUNK)
            cp = pltpu.make_async_copy(mask_ref.at[:, pl.ds(off, CHUNK)], m_loc.at[par, xx], sems.at[par * 4 + xx])
            cp.start()
            loads.append((par, xx, cp))
    lanes = jnp.zeros((USERS, LANE), F32)
    for par, xx, cp in loads:
        cp.wait()
        m = m_loc[par, xx].astype(F32)
        (other_ref if par else own_ref)[xx] = m.astype(BF16)
        di_ref[par, :, xx * CHUNK:(xx + 1) * CHUNK] = jnp.sum(m, axis=0, keepdims=True)
        for g in range(4):
            lanes = lanes + m[:, g * LANE:(g + 1) * LANE]
    rows = lax.dot_general(jnp.ones((8, LANE), BF16), lanes.astype(BF16), (((1,), (1,)), ((), ())),
                           preferred_element_type=F32)
    du_ref[...] = rows[0:1]


S_MASK, S_DU, S_DI, S_FIN, S_EU, S_D, S_SZ, S_LOSS = range(8)
S_UAG = S_LOSS + 1
S_IAG = S_UAG + NUM_LAYERS
S_URS = S_IAG + NUM_LAYERS
S_IRS = S_URS + NUM_LAYERS
N_SEM = S_IRS + NUM_LAYERS


def far_first(*sizes):
    offsets = [()]
    for size in sizes:
        offsets = [o + (d,) for o in offsets for d in range(size)]
    hops = lambda o: sum(min(d, n - d) for d, n in zip(o[:-1], sizes)) * 2 + o[-1]
    return sorted(offsets[1:], key=hops, reverse=True)


def main_kernel(own_ref, other_ref, du_ref, di_ref, ut_v, it_v, tr_ref, ou_ref, oi_ref, ol_ref,
                rem, adj, du, di, uag, iag, usend, urecv, isend, irecv, utp, ei, fin, acc_i,
                eu, wmat, umat, dsend, drecv, sz, lag, send_sem, recv_sem):
    e, c, r, x, k = place()
    q = k * COLS + c * 4 + e
    b = r * 4 + c
    links = Links(send_sem, recv_sem)
    send, wait_recv, wait_send = links.send, links.wait_recv, links.wait_send
    es = [lax.rem(e + d, 4) for d in range(4)]
    cs = [lax.rem(c + d, 4) for d in range(4)]
    xs = [lax.rem(x + d, 4) for d in range(4)]
    ks = [k, 1 - k]
    partner = device(2 * x + ks[1], c, e)
    q_peers = [(ks[dk] * COLS + cs[dc] * 4 + es[de], device(2 * x + ks[dk], cs[dc], es[de]))
               for dc, de, dk in far_first(4, 4, 2)]
    b_peers = [((2 * xs[dx] + ks[dk]) * 4 + cs[dc], device(2 * xs[dx] + ks[dk], cs[dc], e))
               for dx, dc, dk in far_first(4, 4, 2)]
    xz_peers = [(es[de], device(2 * xs[dx] + k, c, es[de])) for dx, de, _ in far_first(4, 4, 1)]

    for _, target in q_peers:
        greet(target)
    for dx in range(1, 4):
        for de in range(4):
            greet(device(2 * xs[dx] + k, c, es[de]))
        greet(device(2 * xs[dx] + ks[1], c, e))
    pl.semaphore_wait(pltpu.get_barrier_semaphore(), OTHERS + 12 + 3)

    for _, target in q_peers:
        send(du_ref, du.at[q], S_DU, target)
    for dx in (2, 1, 3, 0):
        for dk in range(2):
            if dx or dk:
                send(di_ref.at[dk], di.at[r], S_DI, device(2 * xs[dx] + ks[dk], c, e))
    send(other_ref, rem, S_MASK, partner)
    lane_lo = lax.broadcasted_iota(jnp.int32, (8, LANE), 1) < EMB
    user0 = ut_v[...].astype(F32)
    packed = jnp.concatenate([user0[0:8], user0[8:16]], axis=1)
    uag[0, q] = packed.astype(BF16)
    acc_u = packed

    def send_uag(layer):
        for _, target in q_peers:
            send(uag.at[layer, q], uag.at[layer, q], S_UAG + layer, target)

    def send_iag(layer):
        for j in (2, 1, 3):
            mine = iag.at[layer % 2, pl.ds(x * 4, 4)]
            send(mine, mine, S_IAG + layer, device(2 * xs[j] + k, c, e))

    for ee, target in xz_peers:
        send(it_v.at[:, pl.ds(pl.multiple_of(ee * CHUNK, CHUNK), CHUNK)], iag.at[0, x * 4 + e], S_IAG, target)
    send_uag(0)
    iag[0, x * 4 + e] = it_v[:, pl.ds(pl.multiple_of(e * CHUNK, CHUNK), CHUNK)]
    du[q] = du_ref[...]
    di[r] = di_ref[0]
    wait_recv(du.at[pl.ds(0, OTHERS)], S_DU)
    wait_recv(di.at[pl.ds(0, 7)], S_DI)

    inv_i = lax.rsqrt(jnp.maximum(jnp.sum(di[...], axis=0), 1.0))

    def build(source, target, core):
        deg = jnp.sum(du[pl.ds(core * COLS, COLS)], axis=0)
        inv_u = lax.rsqrt(jnp.maximum(deg, 1.0))
        for rc in range(2):
            rows = slice(rc * LANE, (rc + 1) * LANE)
            col = jnp.broadcast_to(inv_u[:, rows], (LANE, LANE)).T
            for xx in range(4):
                m = source[xx, rows, :].astype(F32)
                for g in range(4):
                    lanes = slice(g * LANE, (g + 1) * LANE)
                    lo = xx * CHUNK + g * LANE
                    target[xx, rows, lanes] = ((col * m[:, lanes]) * inv_i[:, lo:lo + LANE]).astype(BF16)

    build(own_ref, adj, ks[0])
    wait_recv(rem, S_MASK)
    build(rem, rem, ks[1])
    parts = ((adj, ks[0]), (rem, ks[1]))

    def item_partials(layer):
        slot = layer % 2
        wait_recv(uag.at[layer, pl.ds(0, OTHERS)], S_UAG + layer)
        for h, (_, core) in enumerate(parts):
            for g in range(2):
                for ee in range(4):
                    s0 = core * COLS + g * 8 + ee
                    top, bot = unpack_half(uag[layer, s0].astype(F32), uag[layer, s0 + 4].astype(F32), lane_lo)
                    both = jnp.concatenate([top, bot], axis=0).astype(BF16)
                    utp[h, ee * COLS:(ee + 1) * COLS, g * LANE:(g + 1) * LANE] = both
        if layer >= 2:
            wait_send(irecv.at[0, pl.ds(0, 3)], S_IRS + layer - 2)
        for j in (2, 1, 3, 0):
            part = jnp.dot(utp[0], adj[xs[j]], preferred_element_type=F32)
            part = part + jnp.dot(utp[1], rem[xs[j]], preferred_element_type=F32)
            if j == 0:
                irecv[slot, x] = part
            else:
                isend[slot, j - 1] = part
                send(isend.at[slot, j - 1], irecv.at[slot, x], S_IRS + layer, device(2 * xs[j] + k, c, e))

    def user_partials(layer):
        slot = layer % 2
        if layer == 0:
            wait_recv(iag.at[0, pl.ds(0, 15)], S_IAG)
        else:
            wait_recv(iag.at[slot, pl.ds(0, 12)], S_IAG + layer)
        if layer >= 1:
            wait_send(usend.at[pl.ds(0, OTHERS)], S_URS + layer - 1)
        for half, core in parts:
            part = jnp.zeros((EMB, USERS), F32)
            for xx in range(4):
                part = part + lax.dot_general(iag[slot, xx * 4:(xx + 1) * 4].reshape(EMB, CHUNK), half[xx],
                                              (((1,), (1,)), ((), ())), preferred_element_type=F32)
            for g in range(2):
                for ee in range(4):
                    s0 = core * COLS + g * 8 + ee
                    v = part[ee * COLS:(ee + 1) * COLS, g * LANE:(g + 1) * LANE]
                    first, second = pack_half(v[0:8], v[8:16], lane_lo)
                    usend[s0] = first
                    usend[s0 + 4] = second
        for qq, target in q_peers:
            send(usend.at[qq], urecv.at[slot, q], S_URS + layer, target)
        urecv[slot, q] = usend[q]

    def next_users(layer):
        wait_recv(urecv.at[layer % 2, pl.ds(0, OTHERS)], S_URS + layer)
        return jnp.sum(urecv[layer % 2], axis=0).astype(BF16)

    def next_items(layer):
        slot = layer % 2
        wait_recv(irecv.at[slot, pl.ds(0, 3)], S_IRS + layer)
        return ((irecv[slot, 0] + irecv[slot, 1]) + (irecv[slot, 2] + irecv[slot, 3])).astype(BF16)

    for layer in range(NUM_LAYERS):
        last = layer + 1 == NUM_LAYERS
        if last:
            item_partials(layer)
            user_partials(layer)
            item_next = next_items(layer)
            item_sum = acc_i[...] + item_next.astype(F32)
        else:
            user_partials(layer)
            if layer == 0:
                acc_i[...] = iag[0, pl.ds(x * 4, 4)].reshape(EMB, CHUNK).astype(F32)
            item_partials(layer)
            user_next = next_users(layer)
            uag[layer + 1, q] = user_next
            send_uag(layer + 1)
            acc_u = acc_u + user_next.astype(F32)
            item_next = next_items(layer)
            iag[(layer + 1) % 2, pl.ds(x * 4, 4)] = item_next.reshape(4, COLS, CHUNK)
            send_iag(layer + 1)
            acc_i[...] = acc_i[...] + item_next.astype(F32)

    ei[...] = (item_sum / (NUM_LAYERS + 1)).astype(BF16)
    for j in (2, 1, 3):
        send(ei.at[pl.ds(pl.multiple_of(es[j] * COLS, COLS), COLS), :], fin.at[e], S_FIN, device(r, c, es[j]))
    fin[e] = ei[pl.ds(pl.multiple_of(e * COLS, COLS), COLS), :]
    acc_u = acc_u + next_users(NUM_LAYERS - 1).astype(F32)
    fin_u = (acc_u / (NUM_LAYERS + 1)).astype(BF16)
    eu[b] = fin_u
    for _, target in b_peers:
        send(eu.at[b], eu.at[b], S_EU, target)
    fin_u = fin_u.astype(F32)
    ou_ref[...] = jnp.concatenate([fin_u[:, 0:EMB], pltpu.roll(fin_u, EMB, 1)[:, 0:EMB]], axis=0).astype(BF16)
    wait_recv(fin.at[pl.ds(0, 3)], S_FIN)
    for h in range(COLS):
        wmat[h * COLS:(h + 1) * COLS, :] = fin[h // 4, :, (h % 4) * LANE:(h % 4 + 1) * LANE]
    first_item = (c * 8 + r) * ITEMS

    def differences(i, carry):
        row = (r + 4 + i) % 8
        ids = tr_ref[:, pl.ds(pl.multiple_of(row * CHUNK, CHUNK), CHUNK)] - first_item
        diff = pick_rows(wmat[...], ids[1:2]) - pick_rows(wmat[...], ids[2:3])
        for g in range(4):
            dsend[row * 4 + g] = diff[:, g * LANE:(g + 1) * LANE]
        for g in range(4):
            @pl.when(row * 4 + g != b)
            def _():
                send(dsend.at[row * 4 + g], drecv.at[b], S_D, device(row, g, e))
        return carry

    lax.fori_loop(0, 8, differences, 0)
    drecv[b] = dsend[b]
    wait_recv(eu.at[pl.ds(0, OTHERS)], S_EU)
    for g in range(COLS):
        top, bot = unpack_half(eu[2 * g].astype(F32), eu[2 * g + 1].astype(F32), lane_lo)
        umat[g * COLS:(g + 1) * COLS, :] = jnp.concatenate([top, bot], axis=0).astype(BF16)
    e_user = pick_rows(umat[...], tr_ref[0:1, pl.ds(pl.multiple_of(b * LANE, LANE), LANE)])
    wait_recv(drecv.at[pl.ds(0, OTHERS)], S_D)
    sz[e] = jnp.sum(e_user * jnp.sum(drecv[...], axis=0), axis=0, keepdims=True)
    for j in (2, 1, 3):
        send(sz.at[e], sz.at[e], S_SZ, device(r, c, es[j]))
    wait_recv(sz.at[pl.ds(0, 3)], S_SZ)
    score = (sz[0] + sz[1]) + (sz[2] + sz[3])
    lag[b] = jnp.maximum(-score, 0.0) + jnp.log1p(jnp.exp(-jnp.abs(score)))
    for _, target in b_peers:
        send(lag.at[b], lag.at[b], S_LOSS, target)
    for s in range(4):
        oi_ref[:, s * CHUNK:(s + 1) * CHUNK] = fin[s]
    wait_send(rem, S_MASK)
    wait_send(du.at[pl.ds(0, OTHERS)], S_DU)
    wait_send(di.at[pl.ds(0, 7)], S_DI)
    for layer in range(NUM_LAYERS):
        wait_send(uag.at[layer, pl.ds(0, OTHERS)], S_UAG + layer)
        if layer == 0:
            wait_send(iag.at[0, pl.ds(0, 15)], S_IAG)
        else:
            wait_send(iag.at[layer % 2, pl.ds(0, 12)], S_IAG + layer)
    wait_send(usend.at[pl.ds(0, OTHERS)], S_URS + NUM_LAYERS - 1)
    for layer in range(NUM_LAYERS - 2, NUM_LAYERS):
        wait_send(irecv.at[0, pl.ds(0, 3)], S_IRS + layer)
    wait_send(fin.at[pl.ds(0, 3)], S_FIN)
    wait_send(eu.at[pl.ds(0, OTHERS)], S_EU)
    wait_send(drecv.at[pl.ds(0, OTHERS)], S_D)
    wait_send(sz.at[pl.ds(0, 3)], S_SZ)
    wait_send(lag.at[pl.ds(0, OTHERS)], S_LOSS)
    wait_recv(lag.at[pl.ds(0, OTHERS)], S_LOSS)
    for s in range(PEERS):
        ol_ref[s:s + 1, :] = lag[s]


def call(body, outs, in_specs, scratch, collective_id=None, vmem_mib=24):
    vmem = pl.BlockSpec(memory_space=pltpu.VMEM)
    return pl.pallas_call(
        body,
        out_shape=tuple(jax.ShapeDtypeStruct(shape, dtype) for shape, dtype in outs),
        in_specs=[vmem if s is None else s for s in in_specs],
        out_specs=(vmem,) * len(outs),
        scratch_shapes=scratch,
        compiler_params=pltpu.CompilerParams(
            collective_id=collective_id, has_side_effects=collective_id is not None,
            vmem_limit_bytes=vmem_mib * 1024 * 1024),
        name=body.__name__)


def solution(mesh):
    vm = pltpu.VMEM
    dma = pltpu.SemaphoreType.DMA

    def local_fn(mask_blk, user_sh, item_sh, triples):
        half = (4, USERS, CHUNK)
        pieces = (PEERS, 8, LANE)
        panel = (EMB, CHUNK)
        own, other, du, di = call(
            load_kernel, [(half, BF16), (half, BF16), ((1, USERS), F32), ((2, 1, ITEMS), F32)],
            [pl.BlockSpec(memory_space=pl.ANY)], [vm((2,) + half, jnp.int32), dma((8,))], vmem_mib=49)(mask_blk)
        out_u, out_i, loss = call(
            main_kernel, [((COLS, EMB), BF16), ((COLS, ITEMS), BF16), ((PEERS, LANE), F32)], [None] * 7,
            [vm(half, BF16), vm(half, BF16), vm((PEERS, 1, USERS), F32), vm((8, 1, ITEMS), F32),
             vm((NUM_LAYERS,) + pieces, BF16), vm((2, 4 * 4, COLS, CHUNK), BF16), vm(pieces, F32),
             vm((2,) + pieces, F32),
             vm((2, 3) + panel, F32), vm((2, 4) + panel, F32), vm((2, EMB, USERS), BF16), vm(panel, BF16),
             vm((4, COLS, CHUNK), BF16), vm(panel, F32),
             vm(pieces, BF16), vm((USERS, LANE), BF16), vm((USERS, LANE), BF16), vm((PEERS, COLS, LANE), F32),
             vm((PEERS, COLS, LANE), F32), vm((4, 1, LANE), F32), vm((PEERS, 1, LANE), F32),
             dma((N_SEM,)), dma((N_SEM,))],
            0)(own, other, du, di, user_sh.T, item_sh.T, triples.T)
        return out_u.T, out_i.T, loss.reshape(PEERS * LANE)

    return jax.shard_map(
        local_fn, mesh=mesh,
        in_specs=(P("row", "col"), P(("row", "col"), "emb"), P(("col", "row"), "emb"), P()),
        out_specs=(P(("row", "col"), "emb"), P(("col", "row"), "emb"), P()),
        check_vma=False)
```

time: 462 us -> 70.9 us (0.15)
  waiting for transfers between devices: 233 us -> 0 us
  blocking collectives: 96.5 us -> 0 us
  Pallas kernels: 0 us -> 68.2 us
  local copies, waits for them, and re-layouts: 49.6 us -> 1.84 us
  matrix products: 32.6 us -> 0 us
  other arithmetic: 31.4 us -> 0 us
  between operations: 14.4 us -> 0.7 us
    psum x2 -> x0, waiting for transfers between devices: 132 us -> none  [the longest x1 104 us: bpr_terms(): fetched = lax.psum(fetched, ('row', 'col'))]
    all_gather x6 -> x0, blocking collectives: 75.3 us -> none  [the longest x3 48.5 us: local_fn(): item_panel = lax.all_gather(item_cur, 'row', axis=0, tiled=True)]
    reduce_scatter x3 -> x0, waiting for transfers between devices: 75.2 us -> none  [local_fn(): lax.psum_scatter(item_part, 'row', scatter_dimension=0, tiled=True)]
    pallas_call x0 -> x2, Pallas kernels: none -> 68.2 us  [the longest x1 65.8 us: local_fn(): call(main_kernel, [((COLS, EMB), BF16), ((COLS, ITEMS), BF16), ((PEERS, L...]
    gather x3 -> x0, local copies, waits for them, and re-layouts: 39.2 us -> none  [lookup_rows(): picked = jnp.take(table, jnp.clip(local_ids, 0, own_rows - 1), axis=0)]
    unnamed x11 -> x0, waiting for transfers between devices: 25.9 us -> none
    psum x2 -> x0, blocking collectives: 21.2 us -> none  [the longest x1 13.3 us: bpr_terms(): score = lax.psum(jnp.sum(e_user * (e_pos - e_neg), axis=1), 'emb')]
    dot_general x3 -> x0, matrix products: 16.9 us -> none  [local_fn(): lax.dot_general(adj_blk, user_panel, (((0,), (0,)), ((), ())), preferred_...]
  transfers between devices with their start and end apart: 8 -> 0, of which waited for: 7 -> 0; matrix products, arithmetic and copies ran while one was open for 12% -> 0% of each run, Pallas kernels for 0% -> 0%
where the time goes in v2:
time: 70.9 us; the launch traced here: 70.8 us
  Pallas kernels  68.2 us (96%)
  local copies, waits for them, and re-layouts  1.84 us (3%)
    pallas_call x1, Pallas kernels, local_fn(): call(main_kernel, [((COLS, EMB), BF16), ((COLS, ITEMS), BF16), ((PEERS, L...  65.8 us
    pallas_call x1, Pallas kernels, local_fn(): call(load_kernel, [(half, BF16), (half, BF16), ((1, USERS), F32), ((2, 1,...  2.45 us
    unnamed x9, local copies, waits for them, and re-layouts  1.84 us

profile of v2, /device:TPU:1, one launch (start us, length us, event | category | flops | bytes accessed | tf_op | source)
XLA Modules:
  0.0 70.8 jit_solution(14492424633303320305)
XLA Ops:
  0.6 0.0 copy-start.1
  0.6 0.0 copy-start
  0.7 0.0 copy-start.2
  0.7 2.5 %load_kernel.1 = (bf16[4,256,512]{2,1,0:T(8,128)(2,1)S(1)}, bf16[4,256,512]{2,1,0:T(8,128)(2,1)S(1)}, f32[1,256]{1,0:T(1,128)S(1)}, f32[2,1,2048]{2,1,0:T(1,128)S(1)}) custom-call(s32[256,16384]{1,0:T(8,128)} %mask_ref.1), custom_call_target="tpu_custom_call" | custom-call | tf_op jit(solution)/shard_map/load_kernel/pallas_call | solution.py:360
  3.1 0.0 copy-done.1
  3.1 0.0 copy-done
  3.1 0.0 copy-done.2
  3.2 65.8 %main_kernel.1 = (bf16[16,64]{1,0:T(8,128)(2,1)S(1)}, bf16[16,2048]{1,0:T(8,128)(2,1)S(1)}, f32[32,128]{1,0:T(8,128)S(1)}) custom-call(bf16[4,256,512]{2,1,0:T(8,128)(2,1)S(1)} %get-tuple-element.10.own_ref, bf16[4,256,512]{2,1,0:T(8,128)(2,1)S(1)} %get-tuple-element.11.other_ref, f32[1,256]{1,0:T(1,128)S(1)} %get-tuple-element.12.du_ref, ...), custom_call_target="tpu_custom_call" | custom-call | tf_op jit(solution)/shard_map/main_kernel/pallas_call | solution.py:363
  68.9 0.6 copy.10
  69.5 0.6 copy.11
  70.2 0.6 copy.12
Async XLA Ops:
  0.6 2.5 %copy-start.1 = (s32[4096,3]{0,1:T(4,128)S(1)}, s32[4096,3]{0,1:T(4,128)}, u32[]{:S(2)}) copy-start(s32[4096,3]{0,1:T(4,128)} %param.7) | copy-start | bytes 147460
  0.6 2.5 %copy-start = (bf16[2048,16]{0,1:T(8,128)(2,1)S(1)}, bf16[2048,16]{0,1:T(8,128)(2,1)}, u32[]{:S(2)}) copy-start(bf16[2048,16]{0,1:T(8,128)(2,1)} %param.6) | copy-start | bytes 196612
  0.7 2.5 %copy-start.2 = (bf16[64,16]{0,1:T(8,128)(2,1)S(1)}, bf16[64,16]{0,1:T(8,128)(2,1)}, u32[]{:S(2)}) copy-start(bf16[64,16]{0,1:T(8,128)(2,1)} %param.5) | copy-start | bytes 6148

commit v3 on v2

--- a/solution.py
+++ b/solution.py
@@ -98,8 +98,8 @@
     du_ref[...] = rows[0:1]
 
 
-S_MASK, S_DU, S_DI, S_FIN, S_EU, S_D, S_SZ, S_LOSS = range(8)
-S_UAG = S_LOSS + 1
+S_MASK, S_DU, S_DI, S_EU, S_D, S_LOSS, S_FIN = range(7)
+S_UAG = S_FIN + NUM_LAYERS
 S_IAG = S_UAG + NUM_LAYERS
 S_URS = S_IAG + NUM_LAYERS
 S_IRS = S_URS + NUM_LAYERS
@@ -115,8 +115,8 @@
 
 
 def main_kernel(own_ref, other_ref, du_ref, di_ref, ut_v, it_v, tr_ref, ou_ref, oi_ref, ol_ref,
-                rem, adj, du, di, uag, iag, usend, urecv, isend, irecv, utp, ei, fin, acc_i,
-                eu, wmat, umat, dsend, drecv, sz, lag, send_sem, recv_sem):
+                rem, adj, du, di, uag, iag, usend, urecv, isend, irecv, utp, ib, frecv, fin,
+                eu, wmat, umat, dsend, drecv, lag, send_sem, recv_sem):
     e, c, r, x, k = place()
     q = k * COLS + c * 4 + e
     b = r * 4 + c
@@ -131,6 +131,7 @@
                for dc, de, dk in far_first(4, 4, 2)]
     b_peers = [((2 * xs[dx] + ks[dk]) * 4 + cs[dc], device(2 * xs[dx] + ks[dk], cs[dc], e))
                for dx, dc, dk in far_first(4, 4, 2)]
+    all_peers = [device(2 * xs[dx] + ks[dk], cs[dc], es[de]) for dx, dc, de, dk in far_first(4, 4, 4, 2)]
     xz_peers = [(es[de], device(2 * xs[dx] + k, c, es[de])) for dx, de, _ in far_first(4, 4, 1)]
 
     for _, target in q_peers:
@@ -202,16 +203,17 @@
                     top, bot = unpack_half(uag[layer, s0].astype(F32), uag[layer, s0 + 4].astype(F32), lane_lo)
                     both = jnp.concatenate([top, bot], axis=0).astype(BF16)
                     utp[h, ee * COLS:(ee + 1) * COLS, g * LANE:(g + 1) * LANE] = both
-        if layer >= 2:
-            wait_send(irecv.at[0, pl.ds(0, 3)], S_IRS + layer - 2)
+        if layer >= 1:
+            wait_send(isend.at[pl.ds(0, 3)], S_IRS + layer - 1)
         for j in (2, 1, 3, 0):
             part = jnp.dot(utp[0], adj[xs[j]], preferred_element_type=F32)
-            part = part + jnp.dot(utp[1], rem[xs[j]], preferred_element_type=F32)
-            if j == 0:
-                irecv[slot, x] = part
-            else:
-                isend[slot, j - 1] = part
-                send(isend.at[slot, j - 1], irecv.at[slot, x], S_IRS + layer, device(2 * xs[j] + k, c, e))
+            isend[j] = (part + jnp.dot(utp[1], rem[xs[j]], preferred_element_type=F32)).reshape(4, COLS, CHUNK)
+            if j and layer + 1 < NUM_LAYERS:
+                send(isend.at[j], irecv.at[slot, j - 1], S_IRS + layer, device(2 * xs[j] + k, c, e))
+            elif layer + 1 == NUM_LAYERS:
+                for de in (2, 1, 3, 0):
+                    if j or de:
+                        send(isend.at[j, es[de]], frecv.at[x * 4 + e], S_IRS + layer, device(2 * xs[j] + k, c, es[de]))
 
     def user_partials(layer):
         slot = layer % 2
@@ -243,42 +245,45 @@
 
     def next_items(layer):
         slot = layer % 2
-        wait_recv(irecv.at[slot, pl.ds(0, 3)], S_IRS + layer)
-        return ((irecv[slot, 0] + irecv[slot, 1]) + (irecv[slot, 2] + irecv[slot, 3])).astype(BF16)
-
-    for layer in range(NUM_LAYERS):
-        last = layer + 1 == NUM_LAYERS
-        if last:
-            item_partials(layer)
-            user_partials(layer)
-            item_next = next_items(layer)
-            item_sum = acc_i[...] + item_next.astype(F32)
-        else:
-            user_partials(layer)
-            if layer == 0:
-                acc_i[...] = iag[0, pl.ds(x * 4, 4)].reshape(EMB, CHUNK).astype(F32)
-            item_partials(layer)
-            user_next = next_users(layer)
-            uag[layer + 1, q] = user_next
-            send_uag(layer + 1)
-            acc_u = acc_u + user_next.astype(F32)
-            item_next = next_items(layer)
-            iag[(layer + 1) % 2, pl.ds(x * 4, 4)] = item_next.reshape(4, COLS, CHUNK)
-            send_iag(layer + 1)
-            acc_i[...] = acc_i[...] + item_next.astype(F32)
-
-    ei[...] = (item_sum / (NUM_LAYERS + 1)).astype(BF16)
-    for j in (2, 1, 3):
-        send(ei.at[pl.ds(pl.multiple_of(es[j] * COLS, COLS), COLS), :], fin.at[e], S_FIN, device(r, c, es[j]))
-    fin[e] = ei[pl.ds(pl.multiple_of(e * COLS, COLS), COLS), :]
-    acc_u = acc_u + next_users(NUM_LAYERS - 1).astype(F32)
+        wait_recv(irecv.at[slot], S_IRS + layer)
+        return ((isend[0] + irecv[slot, 0]) + (irecv[slot, 1] + irecv[slot, 2])).astype(BF16)
+
+    for layer in range(NUM_LAYERS - 1):
+        item_partials(layer)
+        user_partials(layer)
+        user_next = next_users(layer)
+        uag[layer + 1, q] = user_next
+        send_uag(layer + 1)
+        acc_u = acc_u + user_next.astype(F32)
+        iag[(layer + 1) % 2, pl.ds(x * 4, 4)] = next_items(layer)
+        send_iag(layer + 1)
+        for j in (2, 1, 3):
+            send(iag.at[(layer + 1) % 2, x * 4 + es[j]], ib.at[layer, e], S_FIN + layer, device(r, c, es[j]))
+        ib[layer, e] = iag[(layer + 1) % 2, x * 4 + e]
+
+    final = NUM_LAYERS - 1
+    item_partials(final)
+    frecv[x * 4 + e] = isend[0, e]
+    user_partials(final)
+    for layer in range(final):
+        wait_recv(ib.at[layer, pl.ds(0, 3)], S_FIN + layer)
+    item_sums = []
+    for s in range(4):
+        item_sum = it_v[:, s * CHUNK:(s + 1) * CHUNK].astype(F32)
+        for layer in range(final):
+            item_sum = item_sum + ib[layer, s].astype(F32)
+        item_sums.append(item_sum)
+    acc_u = acc_u + next_users(final).astype(F32)
     fin_u = (acc_u / (NUM_LAYERS + 1)).astype(BF16)
     eu[b] = fin_u
     for _, target in b_peers:
         send(eu.at[b], eu.at[b], S_EU, target)
     fin_u = fin_u.astype(F32)
     ou_ref[...] = jnp.concatenate([fin_u[:, 0:EMB], pltpu.roll(fin_u, EMB, 1)[:, 0:EMB]], axis=0).astype(BF16)
-    wait_recv(fin.at[pl.ds(0, 3)], S_FIN)
+    wait_recv(frecv.at[pl.ds(0, 15)], S_IRS + final)
+    for s in range(4):
+        item_next = ((frecv[s] + frecv[4 + s]) + (frecv[4 * 2 + s] + frecv[4 * 3 + s])).astype(BF16)
+        fin[s] = ((item_sums[s] + item_next.astype(F32)) / (NUM_LAYERS + 1)).astype(BF16)
     for h in range(COLS):
         wmat[h * COLS:(h + 1) * COLS, :] = fin[h // 4, :, (h % 4) * LANE:(h % 4 + 1) * LANE]
     first_item = (c * 8 + r) * ITEMS
@@ -303,14 +308,10 @@
         umat[g * COLS:(g + 1) * COLS, :] = jnp.concatenate([top, bot], axis=0).astype(BF16)
     e_user = pick_rows(umat[...], tr_ref[0:1, pl.ds(pl.multiple_of(b * LANE, LANE), LANE)])
     wait_recv(drecv.at[pl.ds(0, OTHERS)], S_D)
-    sz[e] = jnp.sum(e_user * jnp.sum(drecv[...], axis=0), axis=0, keepdims=True)
-    for j in (2, 1, 3):
-        send(sz.at[e], sz.at[e], S_SZ, device(r, c, es[j]))
-    wait_recv(sz.at[pl.ds(0, 3)], S_SZ)
-    score = (sz[0] + sz[1]) + (sz[2] + sz[3])
-    lag[b] = jnp.maximum(-score, 0.0) + jnp.log1p(jnp.exp(-jnp.abs(score)))
-    for _, target in b_peers:
-        send(lag.at[b], lag.at[b], S_LOSS, target)
+    mine = e * PEERS + b
+    lag[mine] = jnp.sum(e_user * jnp.sum(drecv[...], axis=0), axis=0, keepdims=True)
+    for target in all_peers:
+        send(lag.at[mine], lag.at[mine], S_LOSS, target)
     for s in range(4):
         oi_ref[:, s * CHUNK:(s + 1) * CHUNK] = fin[s]
     wait_send(rem, S_MASK)
@@ -323,25 +324,34 @@
         else:
             wait_send(iag.at[layer % 2, pl.ds(0, 12)], S_IAG + layer)
     wait_send(usend.at[pl.ds(0, OTHERS)], S_URS + NUM_LAYERS - 1)
-    for layer in range(NUM_LAYERS - 2, NUM_LAYERS):
-        wait_send(irecv.at[0, pl.ds(0, 3)], S_IRS + layer)
-    wait_send(fin.at[pl.ds(0, 3)], S_FIN)
+    wait_send(frecv.at[pl.ds(0, 15)], S_IRS + final)
+    for layer in range(final):
+        wait_send(ib.at[layer, pl.ds(0, 3)], S_FIN + layer)
     wait_send(eu.at[pl.ds(0, OTHERS)], S_EU)
     wait_send(drecv.at[pl.ds(0, OTHERS)], S_D)
-    wait_send(sz.at[pl.ds(0, 3)], S_SZ)
-    wait_send(lag.at[pl.ds(0, OTHERS)], S_LOSS)
-    wait_recv(lag.at[pl.ds(0, OTHERS)], S_LOSS)
+    wait_send(lag.at[pl.ds(0, 4 * PEERS - 1)], S_LOSS)
+    wait_recv(lag.at[pl.ds(0, 4 * PEERS - 1)], S_LOSS)
     for s in range(PEERS):
-        ol_ref[s:s + 1, :] = lag[s]
-
-
-def call(body, outs, in_specs, scratch, collective_id=None, vmem_mib=24):
+        ol_ref[s:s + 1, :] = (lag[s] + lag[s + PEERS]) + (lag[s + 2 * PEERS] + lag[s + 3 * PEERS])
+    score = ol_ref[...]
+    ol_ref[...] = jnp.maximum(-score, 0.0) + jnp.log1p(jnp.exp(-jnp.abs(score)))
+
+
+def emit_kernel(ou, oi, ol, ou_ref, oi_ref, ol_ref, sems):
+    copies = [pltpu.make_async_copy(a, b, sems.at[i]) for i, (a, b) in enumerate(((oi, oi_ref), (ou, ou_ref), (ol, ol_ref)))]
+    for cp in copies:
+        cp.start()
+    for cp in copies:
+        cp.wait()
+
+
+def call(body, outs, in_specs, scratch, collective_id=None, vmem_mib=24, out_spec=None):
     vmem = pl.BlockSpec(memory_space=pltpu.VMEM)
     return pl.pallas_call(
         body,
         out_shape=tuple(jax.ShapeDtypeStruct(shape, dtype) for shape, dtype in outs),
         in_specs=[vmem if s is None else s for s in in_specs],
-        out_specs=(vmem,) * len(outs),
+        out_specs=(out_spec or vmem,) * len(outs),
         scratch_shapes=scratch,
         compiler_params=pltpu.CompilerParams(
             collective_id=collective_id, has_side_effects=collective_id is not None,
@@ -356,21 +366,23 @@
     def local_fn(mask_blk, user_sh, item_sh, triples):
         half = (4, USERS, CHUNK)
         pieces = (PEERS, 8, LANE)
-        panel = (EMB, CHUNK)
+        chunk = (4, COLS, CHUNK)
         own, other, du, di = call(
             load_kernel, [(half, BF16), (half, BF16), ((1, USERS), F32), ((2, 1, ITEMS), F32)],
             [pl.BlockSpec(memory_space=pl.ANY)], [vm((2,) + half, jnp.int32), dma((8,))], vmem_mib=49)(mask_blk)
-        out_u, out_i, loss = call(
-            main_kernel, [((COLS, EMB), BF16), ((COLS, ITEMS), BF16), ((PEERS, LANE), F32)], [None] * 7,
+        results = [((COLS, EMB), BF16), ((COLS, ITEMS), BF16), ((PEERS, LANE), F32)]
+        made = call(
+            main_kernel, results, [None] * 7,
             [vm(half, BF16), vm(half, BF16), vm((PEERS, 1, USERS), F32), vm((8, 1, ITEMS), F32),
              vm((NUM_LAYERS,) + pieces, BF16), vm((2, 4 * 4, COLS, CHUNK), BF16), vm(pieces, F32),
              vm((2,) + pieces, F32),
-             vm((2, 3) + panel, F32), vm((2, 4) + panel, F32), vm((2, EMB, USERS), BF16), vm(panel, BF16),
-             vm((4, COLS, CHUNK), BF16), vm(panel, F32),
+             vm((4,) + chunk, F32), vm((2, 3) + chunk, F32), vm((2, EMB, USERS), BF16),
+             vm((NUM_LAYERS - 1,) + chunk, BF16), vm((4 * 4, COLS, CHUNK), F32), vm(chunk, BF16),
              vm(pieces, BF16), vm((USERS, LANE), BF16), vm((USERS, LANE), BF16), vm((PEERS, COLS, LANE), F32),
-             vm((PEERS, COLS, LANE), F32), vm((4, 1, LANE), F32), vm((PEERS, 1, LANE), F32),
+             vm((PEERS, COLS, LANE), F32), vm((4 * PEERS, 1, LANE), F32),
              dma((N_SEM,)), dma((N_SEM,))],
             0)(own, other, du, di, user_sh.T, item_sh.T, triples.T)
+        out_u, out_i, loss = call(emit_kernel, results, [None] * 3, [dma((3,))], out_spec=pl.BlockSpec(memory_space=pl.ANY))(*made)
         return out_u.T, out_i.T, loss.reshape(PEERS * LANE)
 
     return jax.shard_map(

time: 70.9 us -> 66.7 us (0.941)
  Pallas kernels: 68.2 us -> 65.8 us
  local copies, waits for them, and re-layouts: 1.84 us -> 0.01 us
    pallas_call x1 -> x2, Pallas kernels: 65.8 us -> 63.4 us  [the longest x1 62.7 us: local_fn(): call(main_kernel, results, [None] * 7, [vm(half, BF16), vm(half, BF16), v...]
    unnamed x9 -> x6, local copies, waits for them, and re-layouts: 1.84 us -> 0.01 us
where the time goes in v3:
time: 66.7 us; the launch traced here: 66.5 us
  Pallas kernels  65.8 us (99%)
  between operations  0.69 us (1%)
    pallas_call x1, Pallas kernels, local_fn(): call(main_kernel, results, [None] * 7, [vm(half, BF16), vm(half, BF16), v...  62.7 us
    pallas_call x1, Pallas kernels, local_fn(): call(load_kernel, [(half, BF16), (half, BF16), ((1, USERS), F32), ((2, 1,...  2.45 us

profile of v3, /device:TPU:1, one launch (start us, length us, event | category | flops | bytes accessed | tf_op | source)
XLA Modules:
  0.0 66.5 jit_solution(4461081360707982448)
XLA Ops:
  0.6 0.0 copy-start.1
  0.6 0.0 copy-start
  0.7 0.0 copy-start.2
  0.7 2.5 %load_kernel.1 = (bf16[4,256,512]{2,1,0:T(8,128)(2,1)S(1)}, bf16[4,256,512]{2,1,0:T(8,128)(2,1)S(1)}, f32[1,256]{1,0:T(1,128)S(1)}, f32[2,1,2048]{2,1,0:T(1,128)S(1)}) custom-call(s32[256,16384]{1,0:T(8,128)} %mask_ref.1), custom_call_target="tpu_custom_call" | custom-call | tf_op jit(solution)/shard_map/load_kernel/pallas_call | solution.py:370
  3.1 0.0 copy-done.1
  3.1 0.0 copy-done
  3.1 0.0 copy-done.2
  3.2 62.7 %main_kernel.1 = (bf16[16,64]{1,0:T(8,128)(2,1)S(1)}, bf16[16,2048]{1,0:T(8,128)(2,1)S(1)}, f32[32,128]{1,0:T(8,128)S(1)}) custom-call(bf16[4,256,512]{2,1,0:T(8,128)(2,1)S(1)} %get-tuple-element.13.own_ref, bf16[4,256,512]{2,1,0:T(8,128)(2,1)S(1)} %get-tuple-element.14.other_ref, f32[1,256]{1,0:T(1,128)S(1)} %get-tuple-element.15.du_ref, ...), custom_call_target="tpu_custom_call" | custom-call | tf_op jit(solution)/shard_map/main_kernel/pallas_call | solution.py:374
  65.9 0.7 emit_kernel.1
Async XLA Ops:
  0.6 2.5 %copy-start.1 = (s32[4096,3]{0,1:T(4,128)S(1)}, s32[4096,3]{0,1:T(4,128)}, u32[]{:S(2)}) copy-start(s32[4096,3]{0,1:T(4,128)} %param.7) | copy-start | bytes 147460
  0.6 2.5 %copy-start = (bf16[2048,16]{0,1:T(8,128)(2,1)S(1)}, bf16[2048,16]{0,1:T(8,128)(2,1)}, u32[]{:S(2)}) copy-start(bf16[2048,16]{0,1:T(8,128)(2,1)} %param.6) | copy-start | bytes 196612
  0.7 2.5 %copy-start.2 = (bf16[64,16]{0,1:T(8,128)(2,1)S(1)}, bf16[64,16]{0,1:T(8,128)(2,1)}, u32[]{:S(2)}) copy-start(bf16[64,16]{0,1:T(8,128)(2,1)} %param.5) | copy-start | bytes 6148

commit v4 on v3

--- a/solution.py
+++ b/solution.py
@@ -33,14 +33,13 @@
 
 def pick_rows(table, ids):
     n = ids.shape[1]
-    low = jnp.bitwise_and(ids, 127)
-    high = lax.shift_right_arithmetic(ids, 7)
-    hot = (lax.broadcasted_iota(jnp.int32, (LANE, n), 0) == low).astype(F32).astype(BF16)
+    low = jnp.bitwise_and(ids, USERS - 1)
+    high = jnp.broadcast_to(lax.shift_right_arithmetic(ids, 8), (COLS, n))
+    hot = (lax.broadcasted_iota(jnp.int32, (USERS, n), 0) == low).astype(F32).astype(BF16)
     wide = jnp.dot(table, hot, preferred_element_type=F32)
-    high16 = jnp.broadcast_to(high, (COLS, n))
     total = jnp.zeros((COLS, n), F32)
-    for blk in range(COLS):
-        total = total + jnp.where(high16 == blk, wide[blk * COLS:(blk + 1) * COLS], 0.0)
+    for blk in range(8):
+        total = jnp.where(high == blk, wide[blk * COLS:(blk + 1) * COLS], total)
     return total
 
 
@@ -182,11 +181,11 @@
             rows = slice(rc * LANE, (rc + 1) * LANE)
             col = jnp.broadcast_to(inv_u[:, rows], (LANE, LANE)).T
             for xx in range(4):
-                m = source[xx, rows, :].astype(F32)
                 for g in range(4):
                     lanes = slice(g * LANE, (g + 1) * LANE)
                     lo = xx * CHUNK + g * LANE
-                    target[xx, rows, lanes] = ((col * m[:, lanes]) * inv_i[:, lo:lo + LANE]).astype(BF16)
+                    m = source[xx, rows, lanes].astype(F32)
+                    target[xx, rows, lanes] = ((col * m) * inv_i[:, lo:lo + LANE]).astype(BF16)
 
     build(own_ref, adj, ks[0])
     wait_recv(rem, S_MASK)
@@ -284,28 +283,24 @@
     for s in range(4):
         item_next = ((frecv[s] + frecv[4 + s]) + (frecv[4 * 2 + s] + frecv[4 * 3 + s])).astype(BF16)
         fin[s] = ((item_sums[s] + item_next.astype(F32)) / (NUM_LAYERS + 1)).astype(BF16)
-    for h in range(COLS):
-        wmat[h * COLS:(h + 1) * COLS, :] = fin[h // 4, :, (h % 4) * LANE:(h % 4 + 1) * LANE]
+    for h in range(8):
+        wmat[h * COLS:(h + 1) * COLS, :] = fin[h // 2, :, (h % 2) * USERS:(h % 2 + 1) * USERS]
     first_item = (c * 8 + r) * ITEMS
 
-    def differences(i, carry):
-        row = (r + 4 + i) % 8
+    for d in (4, 3, 5, 2, 6, 1, 7, 0):
+        row = lax.rem(r + d, 8)
         ids = tr_ref[:, pl.ds(pl.multiple_of(row * CHUNK, CHUNK), CHUNK)] - first_item
         diff = pick_rows(wmat[...], ids[1:2]) - pick_rows(wmat[...], ids[2:3])
         for g in range(4):
             dsend[row * 4 + g] = diff[:, g * LANE:(g + 1) * LANE]
-        for g in range(4):
-            @pl.when(row * 4 + g != b)
-            def _():
-                send(dsend.at[row * 4 + g], drecv.at[b], S_D, device(row, g, e))
-        return carry
-
-    lax.fori_loop(0, 8, differences, 0)
+        for j in (2, 1, 3, 0):
+            if d or j:
+                send(dsend.at[row * 4 + cs[j]], drecv.at[b], S_D, device(row, cs[j], e))
     drecv[b] = dsend[b]
     wait_recv(eu.at[pl.ds(0, OTHERS)], S_EU)
     for g in range(COLS):
         top, bot = unpack_half(eu[2 * g].astype(F32), eu[2 * g + 1].astype(F32), lane_lo)
-        umat[g * COLS:(g + 1) * COLS, :] = jnp.concatenate([top, bot], axis=0).astype(BF16)
+        umat[g // 2 * COLS:(g // 2 + 1) * COLS, g % 2 * LANE:(g % 2 + 1) * LANE] = jnp.concatenate([top, bot], axis=0).astype(BF16)
     e_user = pick_rows(umat[...], tr_ref[0:1, pl.ds(pl.multiple_of(b * LANE, LANE), LANE)])
     wait_recv(drecv.at[pl.ds(0, OTHERS)], S_D)
     mine = e * PEERS + b
@@ -378,7 +373,7 @@
              vm((2,) + pieces, F32),
              vm((4,) + chunk, F32), vm((2, 3) + chunk, F32), vm((2, EMB, USERS), BF16),
              vm((NUM_LAYERS - 1,) + chunk, BF16), vm((4 * 4, COLS, CHUNK), F32), vm(chunk, BF16),
-             vm(pieces, BF16), vm((USERS, LANE), BF16), vm((USERS, LANE), BF16), vm((PEERS, COLS, LANE), F32),
+             vm(pieces, BF16), vm((LANE, USERS), BF16), vm((LANE, USERS), BF16), vm((PEERS, COLS, LANE), F32),
              vm((PEERS, COLS, LANE), F32), vm((4 * PEERS, 1, LANE), F32),
              dma((N_SEM,)), dma((N_SEM,))],
             0)(own, other, du, di, user_sh.T, item_sh.T, triples.T)

time: 66.7 us -> 65.2 us (0.978)
  Pallas kernels: 65.8 us -> 64.4 us
    pallas_call x1, Pallas kernels: 62.7 us -> 61.3 us  [local_fn(): call(main_kernel, results, [None] * 7, [vm(half, BF16), vm(half, BF16), v...]
where the time goes in v4:
time: 65.2 us; the launch traced here: 65.1 us
  Pallas kernels  64.4 us (99%)
  between operations  0.69 us (1%)
    pallas_call x1, Pallas kernels, local_fn(): call(main_kernel, results, [None] * 7, [vm(half, BF16), vm(half, BF16), v...  61.3 us
    pallas_call x1, Pallas kernels, local_fn(): call(load_kernel, [(half, BF16), (half, BF16), ((1, USERS), F32), ((2, 1,...  2.45 us

profile of v4, /device:TPU:1, one launch (start us, length us, event | category | flops | bytes accessed | tf_op | source)
XLA Modules:
  0.0 65.1 jit_solution(14287532848229082727)
XLA Ops:
  0.6 0.0 copy-start.1
  0.6 0.0 copy-start
  0.7 0.0 copy-start.2
  0.7 2.5 %load_kernel.1 = (bf16[4,256,512]{2,1,0:T(8,128)(2,1)S(1)}, bf16[4,256,512]{2,1,0:T(8,128)(2,1)S(1)}, f32[1,256]{1,0:T(1,128)S(1)}, f32[2,1,2048]{2,1,0:T(1,128)S(1)}) custom-call(s32[256,16384]{1,0:T(8,128)} %mask_ref.1), custom_call_target="tpu_custom_call" | custom-call | tf_op jit(solution)/shard_map/load_kernel/pallas_call | solution.py:365
  3.1 0.0 copy-done.1
  3.1 0.0 copy-done
  3.1 0.0 copy-done.2
  3.2 61.3 %main_kernel.1 = (bf16[16,64]{1,0:T(8,128)(2,1)S(1)}, bf16[16,2048]{1,0:T(8,128)(2,1)S(1)}, f32[32,128]{1,0:T(8,128)S(1)}) custom-call(bf16[4,256,512]{2,1,0:T(8,128)(2,1)S(1)} %get-tuple-element.13.own_ref, bf16[4,256,512]{2,1,0:T(8,128)(2,1)S(1)} %get-tuple-element.14.other_ref, f32[1,256]{1,0:T(1,128)S(1)} %get-tuple-element.15.du_ref, ...), custom_call_target="tpu_custom_call" | custom-call | tf_op jit(solution)/shard_map/main_kernel/pallas_call | solution.py:369
  64.5 0.7 %emit_kernel.1 = (bf16[16,64]{1,0:T(8,128)(2,1)}, bf16[16,2048]{1,0:T(8,128)(2,1)}, f32[32,128]{1,0:T(8,128)}) custom-call(bf16[16,64]{1,0:T(8,128)(2,1)S(1)} %get-tuple-element.17.ou, bf16[16,2048]{1,0:T(8,128)(2,1)S(1)} %get-tuple-element.18.oi, f32[32,128]{1,0:T(8,128)S(1)} %get-tuple-element.19.ol), custom_call_target="tpu_custom_call" | custom-call | tf_op jit(solution)/shard_map/emit_kernel/pallas_call | solution.py:380
Async XLA Ops:
  0.6 2.5 %copy-start.1 = (s32[4096,3]{0,1:T(4,128)S(1)}, s32[4096,3]{0,1:T(4,128)}, u32[]{:S(2)}) copy-start(s32[4096,3]{0,1:T(4,128)} %param.7) | copy-start | bytes 147460
  0.6 2.5 %copy-start = (bf16[2048,16]{0,1:T(8,128)(2,1)S(1)}, bf16[2048,16]{0,1:T(8,128)(2,1)}, u32[]{:S(2)}) copy-start(bf16[2048,16]{0,1:T(8,128)(2,1)} %param.6) | copy-start | bytes 196612
  0.7 2.5 %copy-start.2 = (bf16[64,16]{0,1:T(8,128)(2,1)S(1)}, bf16[64,16]{0,1:T(8,128)(2,1)}, u32[]{:S(2)}) copy-start(bf16[64,16]{0,1:T(8,128)(2,1)} %param.5) | copy-start | bytes 6148

commit v5 on v4

--- a/solution.py
+++ b/solution.py
@@ -74,29 +74,6 @@
     pl.semaphore_signal(pltpu.get_barrier_semaphore(), inc=1, device_id=target, device_id_type=MESH)
 
 
-def load_kernel(mask_ref, own_ref, other_ref, du_ref, di_ref, m_loc, sems):
-    e, c, r, x, k = place()
-    loads = []
-    for par in (1, 0):
-        for xx in range(4):
-            row = 2 * xx + jnp.bitwise_xor(k, par)
-            off = pl.multiple_of(row * ITEMS + e * CHUNK, CHUNK)
-            cp = pltpu.make_async_copy(mask_ref.at[:, pl.ds(off, CHUNK)], m_loc.at[par, xx], sems.at[par * 4 + xx])
-            cp.start()
-            loads.append((par, xx, cp))
-    lanes = jnp.zeros((USERS, LANE), F32)
-    for par, xx, cp in loads:
-        cp.wait()
-        m = m_loc[par, xx].astype(F32)
-        (other_ref if par else own_ref)[xx] = m.astype(BF16)
-        di_ref[par, :, xx * CHUNK:(xx + 1) * CHUNK] = jnp.sum(m, axis=0, keepdims=True)
-        for g in range(4):
-            lanes = lanes + m[:, g * LANE:(g + 1) * LANE]
-    rows = lax.dot_general(jnp.ones((8, LANE), BF16), lanes.astype(BF16), (((1,), (1,)), ((), ())),
-                           preferred_element_type=F32)
-    du_ref[...] = rows[0:1]
-
-
 S_MASK, S_DU, S_DI, S_EU, S_D, S_LOSS, S_FIN = range(7)
 S_UAG = S_FIN + NUM_LAYERS
 S_IAG = S_UAG + NUM_LAYERS
@@ -113,10 +90,21 @@
     return sorted(offsets[1:], key=hops, reverse=True)
 
 
-def main_kernel(own_ref, other_ref, du_ref, di_ref, ut_v, it_v, tr_ref, ou_ref, oi_ref, ol_ref,
-                rem, adj, du, di, uag, iag, usend, urecv, isend, irecv, utp, ib, frecv, fin,
-                eu, wmat, umat, dsend, drecv, lag, send_sem, recv_sem):
+def main_kernel(mask_ref, ut_ref, it_ref, tri_ref, ou_ref, oi_ref, ol_ref, ut_v, it_v, tr_ref, small_sem, m_loc, other, rem, adj, du, di_own, di, uag, iag, usend, urecv, isend, irecv, utp, ib, frecv, fin,
+                eu, wmat, umat, dsend, drecv, lag, load_sem, send_sem, recv_sem):
     e, c, r, x, k = place()
+
+    def load(par, xx):
+        row = 2 * xx + (k + par) % 2
+        off = pl.multiple_of(row * ITEMS + e * CHUNK, CHUNK)
+        return pltpu.make_async_copy(mask_ref.at[:, pl.ds(off, CHUNK)], m_loc.at[xx], load_sem.at[par, xx])
+
+    for xx in range(4):
+        load(1, xx).start()
+    small = [pltpu.make_async_copy(a, v, small_sem.at[i])
+             for i, (a, v) in enumerate(((ut_ref, ut_v), (it_ref, it_v), (tri_ref, tr_ref)))]
+    for cp in small:
+        cp.start()
     q = k * COLS + c * 4 + e
     b = r * 4 + c
     links = Links(send_sem, recv_sem)
@@ -139,16 +127,37 @@
         for de in range(4):
             greet(device(2 * xs[dx] + k, c, es[de]))
         greet(device(2 * xs[dx] + ks[1], c, e))
+
+    lanes = jnp.zeros((USERS, LANE), F32)
+    for par in (1, 0):
+        for xx in range(4):
+            load(par, xx).wait()
+            sums = []
+            for g in range(4):
+                at = slice(g * LANE, (g + 1) * LANE)
+                part = m_loc[xx, :, at].astype(F32)
+                (other if par else adj)[xx, :, at] = part.astype(BF16)
+                lo = xx * CHUNK + g * LANE
+                di_own[par, :, lo:lo + LANE] = jnp.sum(part, axis=0, keepdims=True)
+                sums.append(part)
+            lanes = lanes + ((sums[0] + sums[1]) + (sums[2] + sums[3]))
+            if par:
+                load(0, xx).start()
+    ones = jnp.ones((8, LANE), BF16)
+    du[q] = lax.dot_general(ones, lanes.astype(BF16), (((1,), (1,)), ((), ())), preferred_element_type=F32)[0:1]
+    di[r] = di_own[0]
     pl.semaphore_wait(pltpu.get_barrier_semaphore(), OTHERS + 12 + 3)
 
     for _, target in q_peers:
-        send(du_ref, du.at[q], S_DU, target)
+        send(du.at[q], du.at[q], S_DU, target)
     for dx in (2, 1, 3, 0):
         for dk in range(2):
             if dx or dk:
-                send(di_ref.at[dk], di.at[r], S_DI, device(2 * xs[dx] + ks[dk], c, e))
-    send(other_ref, rem, S_MASK, partner)
+                send(di_own.at[dk], di.at[r], S_DI, device(2 * xs[dx] + ks[dk], c, e))
+    send(other, rem, S_MASK, partner)
     lane_lo = lax.broadcasted_iota(jnp.int32, (8, LANE), 1) < EMB
+    for cp in small:
+        cp.wait()
     user0 = ut_v[...].astype(F32)
     packed = jnp.concatenate([user0[0:8], user0[8:16]], axis=1)
     uag[0, q] = packed.astype(BF16)
@@ -167,8 +176,6 @@
         send(it_v.at[:, pl.ds(pl.multiple_of(ee * CHUNK, CHUNK), CHUNK)], iag.at[0, x * 4 + e], S_IAG, target)
     send_uag(0)
     iag[0, x * 4 + e] = it_v[:, pl.ds(pl.multiple_of(e * CHUNK, CHUNK), CHUNK)]
-    du[q] = du_ref[...]
-    di[r] = di_ref[0]
     wait_recv(du.at[pl.ds(0, OTHERS)], S_DU)
     wait_recv(di.at[pl.ds(0, 7)], S_DI)
 
@@ -187,7 +194,7 @@
                     m = source[xx, rows, lanes].astype(F32)
                     target[xx, rows, lanes] = ((col * m) * inv_i[:, lo:lo + LANE]).astype(BF16)
 
-    build(own_ref, adj, ks[0])
+    build(adj, adj, ks[0])
     wait_recv(rem, S_MASK)
     build(rem, rem, ks[1])
     parts = ((adj, ks[0]), (rem, ks[1]))
@@ -362,21 +369,20 @@
         half = (4, USERS, CHUNK)
         pieces = (PEERS, 8, LANE)
         chunk = (4, COLS, CHUNK)
-        own, other, du, di = call(
-            load_kernel, [(half, BF16), (half, BF16), ((1, USERS), F32), ((2, 1, ITEMS), F32)],
-            [pl.BlockSpec(memory_space=pl.ANY)], [vm((2,) + half, jnp.int32), dma((8,))], vmem_mib=49)(mask_blk)
         results = [((COLS, EMB), BF16), ((COLS, ITEMS), BF16), ((PEERS, LANE), F32)]
         made = call(
-            main_kernel, results, [None] * 7,
-            [vm(half, BF16), vm(half, BF16), vm((PEERS, 1, USERS), F32), vm((8, 1, ITEMS), F32),
+            main_kernel, results, [pl.BlockSpec(memory_space=pl.ANY)] * 4,
+            [vm((COLS, EMB), BF16), vm((COLS, ITEMS), BF16), vm((3, PEERS * LANE), jnp.int32), dma((3,)),
+             vm(half, jnp.int32), vm(half, BF16), vm(half, BF16), vm(half, BF16), vm((PEERS, 1, USERS), F32),
+             vm((2, 1, ITEMS), F32), vm((8, 1, ITEMS), F32),
              vm((NUM_LAYERS,) + pieces, BF16), vm((2, 4 * 4, COLS, CHUNK), BF16), vm(pieces, F32),
              vm((2,) + pieces, F32),
              vm((4,) + chunk, F32), vm((2, 3) + chunk, F32), vm((2, EMB, USERS), BF16),
              vm((NUM_LAYERS - 1,) + chunk, BF16), vm((4 * 4, COLS, CHUNK), F32), vm(chunk, BF16),
              vm(pieces, BF16), vm((LANE, USERS), BF16), vm((LANE, USERS), BF16), vm((PEERS, COLS, LANE), F32),
              vm((PEERS, COLS, LANE), F32), vm((4 * PEERS, 1, LANE), F32),
-             dma((N_SEM,)), dma((N_SEM,))],
-            0)(own, other, du, di, user_sh.T, item_sh.T, triples.T)
+             dma((2, 4)), dma((N_SEM,)), dma((N_SEM,))],
+            0, vmem_mib=40)(*(pltpu.with_memory_space_constraint(a, pltpu.HBM) for a in (mask_blk, user_sh.T, item_sh.T, triples.T)))
         out_u, out_i, loss = call(emit_kernel, results, [None] * 3, [dma((3,))], out_spec=pl.BlockSpec(memory_space=pl.ANY))(*made)
         return out_u.T, out_i.T, loss.reshape(PEERS * LANE)
 

time: 65.2 us -> 63.2 us (0.969)
  Pallas kernels: 64.4 us -> 62.4 us
    pallas_call x2 -> x1, Pallas kernels: 63.7 us -> 61.7 us  [local_fn(): call(main_kernel, results, [pl.BlockSpec(memory_space=pl.ANY)] * 4, [vm((...]
where the time goes in v5:
time: 63.2 us; the launch traced here: 63 us
  Pallas kernels  62.4 us (99%)
  between operations  0.64 us (1%)
    pallas_call x1, Pallas kernels, local_fn(): call(main_kernel, results, [pl.BlockSpec(memory_space=pl.ANY)] * 4, [vm((...  61.7 us

profile of v5, /device:TPU:1, one launch (start us, length us, event | category | flops | bytes accessed | tf_op | source)
XLA Modules:
  0.0 63.0 jit_solution(5318769938575114062)
XLA Ops:
  0.6 61.7 %main_kernel.1 = (bf16[16,64]{1,0:T(8,128)(2,1)S(1)}, bf16[16,2048]{1,0:T(8,128)(2,1)S(1)}, f32[32,128]{1,0:T(8,128)S(1)}) custom-call(s32[256,16384]{1,0:T(8,128)} %mask_ref.1, bf16[16,64]{1,0:T(8,128)(2,1)} %bitcast.8, bf16[16,2048]{1,0:T(8,128)(2,1)} %bitcast.6, s32[3,4096]{1,0:T(4,128)} %bitcast.7), custom_call_target="tpu_custom_call" | custom-call | tf_op jit(solution)/shard_map/main_kernel/pallas_call | solution.py:373
  62.4 0.7 %emit_kernel.1 = (bf16[16,64]{1,0:T(8,128)(2,1)}, bf16[16,2048]{1,0:T(8,128)(2,1)}, f32[32,128]{1,0:T(8,128)}) custom-call(bf16[16,64]{1,0:T(8,128)(2,1)S(1)} %get-tuple-element.9.ou, bf16[16,2048]{1,0:T(8,128)(2,1)S(1)} %get-tuple-element.10.oi, f32[32,128]{1,0:T(8,128)S(1)} %get-tuple-element.11.ol), custom_call_target="tpu_custom_call" | custom-call | tf_op jit(solution)/shard_map/emit_kernel/pallas_call | solution.py:386

commit v6 on v5

--- a/solution.py
+++ b/solution.py
@@ -77,7 +77,7 @@
 S_MASK, S_DU, S_DI, S_EU, S_D, S_LOSS, S_FIN = range(7)
 S_UAG = S_FIN + NUM_LAYERS
 S_IAG = S_UAG + NUM_LAYERS
-S_URS = S_IAG + NUM_LAYERS
+S_URS = S_IAG + 4 * NUM_LAYERS
 S_IRS = S_URS + NUM_LAYERS
 N_SEM = S_IRS + NUM_LAYERS
 
@@ -168,9 +168,9 @@
             send(uag.at[layer, q], uag.at[layer, q], S_UAG + layer, target)
 
     def send_iag(layer):
-        for j in (2, 1, 3):
+        for j in (1, 3, 2):
             mine = iag.at[layer % 2, pl.ds(x * 4, 4)]
-            send(mine, mine, S_IAG + layer, device(2 * xs[j] + k, c, e))
+            send(mine, mine, S_IAG + 4 * layer + j, device(2 * xs[j] + k, c, e))
 
     for ee, target in xz_peers:
         send(it_v.at[:, pl.ds(pl.multiple_of(ee * CHUNK, CHUNK), CHUNK)], iag.at[0, x * 4 + e], S_IAG, target)
@@ -211,7 +211,7 @@
                     utp[h, ee * COLS:(ee + 1) * COLS, g * LANE:(g + 1) * LANE] = both
         if layer >= 1:
             wait_send(isend.at[pl.ds(0, 3)], S_IRS + layer - 1)
-        for j in (2, 1, 3, 0):
+        for j in (1, 3, 2, 0):
             part = jnp.dot(utp[0], adj[xs[j]], preferred_element_type=F32)
             isend[j] = (part + jnp.dot(utp[1], rem[xs[j]], preferred_element_type=F32)).reshape(4, COLS, CHUNK)
             if j and layer + 1 < NUM_LAYERS:
@@ -225,15 +225,16 @@
         slot = layer % 2
         if layer == 0:
             wait_recv(iag.at[0, pl.ds(0, 15)], S_IAG)
-        else:
-            wait_recv(iag.at[slot, pl.ds(0, 12)], S_IAG + layer)
         if layer >= 1:
             wait_send(usend.at[pl.ds(0, OTHERS)], S_URS + layer - 1)
-        for half, core in parts:
-            part = jnp.zeros((EMB, USERS), F32)
-            for xx in range(4):
-                part = part + lax.dot_general(iag[slot, xx * 4:(xx + 1) * 4].reshape(EMB, CHUNK), half[xx],
-                                              (((1,), (1,)), ((), ())), preferred_element_type=F32)
+        made = [jnp.zeros((EMB, USERS), F32) for _ in parts]
+        for j in (0, 1, 3, 2):
+            if layer and j:
+                wait_recv(iag.at[slot, pl.ds(0, 4)], S_IAG + 4 * layer + 4 - j)
+            panel = iag[slot, pl.ds(xs[j] * 4, 4)].reshape(EMB, CHUNK)
+            for h, (half, _) in enumerate(parts):
+                made[h] = made[h] + lax.dot_general(panel, half[xs[j]], (((1,), (1,)), ((), ())), preferred_element_type=F32)
+        for part, (_, core) in zip(made, parts):
             for g in range(2):
                 for ee in range(4):
                     s0 = core * COLS + g * 8 + ee
@@ -324,7 +325,8 @@
         if layer == 0:
             wait_send(iag.at[0, pl.ds(0, 15)], S_IAG)
         else:
-            wait_send(iag.at[layer % 2, pl.ds(0, 12)], S_IAG + layer)
+            for j in range(1, 4):
+                wait_send(iag.at[layer % 2, pl.ds(0, 4)], S_IAG + 4 * layer + j)
     wait_send(usend.at[pl.ds(0, OTHERS)], S_URS + NUM_LAYERS - 1)
     wait_send(frecv.at[pl.ds(0, 15)], S_IRS + final)
     for layer in range(final):

time: 63.2 us -> 62.4 us (0.987)
  Pallas kernels: 62.4 us -> 61.6 us
    pallas_call x1, Pallas kernels: 61.7 us -> 60.9 us  [local_fn(): call(main_kernel, results, [pl.BlockSpec(memory_space=pl.ANY)] * 4, [vm((...]
where the time goes in v6:
time: 62.4 us; the launch traced here: 62.2 us
  Pallas kernels  61.6 us (99%)
  between operations  0.64 us (1%)
    pallas_call x1, Pallas kernels, local_fn(): call(main_kernel, results, [pl.BlockSpec(memory_space=pl.ANY)] * 4, [vm((...  60.9 us

profile of v6, /device:TPU:1, one launch (start us, length us, event | category | flops | bytes accessed | tf_op | source)
XLA Modules:
  0.0 62.2 jit_solution(5539192412305414500)
XLA Ops:
  0.6 60.9 %main_kernel.1 = (bf16[16,64]{1,0:T(8,128)(2,1)S(1)}, bf16[16,2048]{1,0:T(8,128)(2,1)S(1)}, f32[32,128]{1,0:T(8,128)S(1)}) custom-call(s32[256,16384]{1,0:T(8,128)} %mask_ref.1, bf16[16,64]{1,0:T(8,128)(2,1)} %bitcast.8, bf16[16,2048]{1,0:T(8,128)(2,1)} %bitcast.6, s32[3,4096]{1,0:T(4,128)} %bitcast.7), custom_call_target="tpu_custom_call" | custom-call | tf_op jit(solution)/shard_map/main_kernel/pallas_call | solution.py:375
  61.5 0.7 %emit_kernel.1 = (bf16[16,64]{1,0:T(8,128)(2,1)}, bf16[16,2048]{1,0:T(8,128)(2,1)}, f32[32,128]{1,0:T(8,128)}) custom-call(bf16[16,64]{1,0:T(8,128)(2,1)S(1)} %get-tuple-element.9.ou, bf16[16,2048]{1,0:T(8,128)(2,1)S(1)} %get-tuple-element.10.oi, f32[32,128]{1,0:T(8,128)S(1)} %get-tuple-element.11.ol), custom_call_target="tpu_custom_call" | custom-call | tf_op jit(solution)/shard_map/emit_kernel/pallas_call | solution.py:388

commit v7 on v6

--- a/solution.py
+++ b/solution.py
@@ -35,7 +35,9 @@
     n = ids.shape[1]
     low = jnp.bitwise_and(ids, USERS - 1)
     high = jnp.broadcast_to(lax.shift_right_arithmetic(ids, 8), (COLS, n))
-    hot = (lax.broadcasted_iota(jnp.int32, (USERS, n), 0) == low).astype(F32).astype(BF16)
+    lanes = lax.broadcasted_iota(jnp.int32, (USERS, n), 0).astype(F32).astype(BF16)
+    same = lanes == low.astype(F32).astype(BF16)
+    hot = jnp.where(same, jnp.ones((), BF16), jnp.zeros((), BF16))
     wide = jnp.dot(table, hot, preferred_element_type=F32)
     total = jnp.zeros((COLS, n), F32)
     for blk in range(8):

time: 62.4 us -> 62.8 us (level)
  no operation moved by 1% of the time
where the time goes in v7:
time: 62.8 us; the launch traced here: 62.7 us
  Pallas kernels  62 us (99%)
  between operations  0.64 us (1%)
    pallas_call x1, Pallas kernels, local_fn(): call(main_kernel, results, [pl.BlockSpec(memory_space=pl.ANY)] * 4, [vm((...  61.4 us

profile of v7, /device:TPU:1, one launch (start us, length us, event | category | flops | bytes accessed | tf_op | source)
XLA Modules:
  0.0 62.7 jit_solution(9208182191708069035)
XLA Ops:
  0.6 61.4 %main_kernel.1 = (bf16[16,64]{1,0:T(8,128)(2,1)S(1)}, bf16[16,2048]{1,0:T(8,128)(2,1)S(1)}, f32[32,128]{1,0:T(8,128)S(1)}) custom-call(s32[256,16384]{1,0:T(8,128)} %mask_ref.1, bf16[16,64]{1,0:T(8,128)(2,1)} %bitcast.8, bf16[16,2048]{1,0:T(8,128)(2,1)} %bitcast.6, s32[3,4096]{1,0:T(4,128)} %bitcast.7), custom_call_target="tpu_custom_call" | custom-call | tf_op jit(solution)/shard_map/main_kernel/pallas_call | solution.py:377
  62.0 0.7 %emit_kernel.1 = (bf16[16,64]{1,0:T(8,128)(2,1)}, bf16[16,2048]{1,0:T(8,128)(2,1)}, f32[32,128]{1,0:T(8,128)}) custom-call(bf16[16,64]{1,0:T(8,128)(2,1)S(1)} %get-tuple-element.9.ou, bf16[16,2048]{1,0:T(8,128)(2,1)S(1)} %get-tuple-element.10.oi, f32[32,128]{1,0:T(8,128)S(1)} %get-tuple-element.11.ol), custom_call_target="tpu_custom_call" | custom-call | tf_op jit(solution)/shard_map/emit_kernel/pallas_call | solution.py:390
